TPU v7x, 32 devices: a whole 2x2x4 slice. The times are simulated.
32 devices in a mesh: dp: 16 (over z, x, core), tensor: 2 (over y).
Axes of the slice: x: 2, y: 2, z: 4, core: 2. Of those that a mesh axis runs over, the one named last changes fastest.
Arguments:
- inputs: bfloat16 [64, 320, 1024], P(('dp', 'tensor')), may hold values from -6 to 6
- lengths: int32 [64], P('dp'), may hold values from 224 to 320, as said below
- cotangent: bfloat16 [64, 320, 1024], P(('dp', 'tensor')), may hold values from -6 to 6
- first_gain: bfloat16 [1024], P(('dp', 'tensor')), may hold values from 0.25 to 1.75
- first_shift: bfloat16 [1024], P(('dp', 'tensor')), may hold values from -2 to 2
- qkv_weight: bfloat16 [3, 1024, 1024], P(None, 'dp', 'tensor'), may hold values from -0.1875 to 0.1875
- query_bias: bfloat16 [1024], P(('dp', 'tensor')), may hold values from -3 to 3
- value_bias: bfloat16 [1024], P(('dp', 'tensor')), may hold values from -3 to 3
- out_weight: bfloat16 [1024, 1024], P('tensor', 'dp'), may hold values from -1.5 to 1.5
- out_bias: bfloat16 [1024], P(('dp', 'tensor')), may hold values from -3 to 3
- second_gain: bfloat16 [1024], P(('dp', 'tensor')), may hold values from 0.25 to 1.75
- second_shift: bfloat16 [1024], P(('dp', 'tensor')), may hold values from -2 to 2
- up_weight: bfloat16 [1024, 4096], P('dp', 'tensor'), may hold values from -0.1875 to 0.1875
- up_bias: bfloat16 [4096], P(('dp', 'tensor')), may hold values from -3 to 3
- down_weight: bfloat16 [4096, 1024], P('tensor', 'dp'), may hold values from -0.09375 to 0.09375
- down_bias: bfloat16 [1024], P(('dp', 'tensor')), may hold values from -3 to 3
Outputs:
- output: bfloat16 [64, 320, 1024], P(('dp', 'tensor'))
- input_grad: float32 [64, 320, 1024], P(('dp', 'tensor'))
- first_gain_grad: float32 [1024], P(('dp', 'tensor'))
- first_shift_grad: float32 [1024], P(('dp', 'tensor'))
- qkv_weight_grad: float32 [3, 1024, 1024], P(None, 'dp', 'tensor')
- query_bias_grad: float32 [1024], P(('dp', 'tensor'))
- value_bias_grad: float32 [1024], P(('dp', 'tensor'))
- out_weight_grad: float32 [1024, 1024], P('tensor', 'dp')
- out_bias_grad: float32 [1024], P(('dp', 'tensor'))
- second_gain_grad: float32 [1024], P(('dp', 'tensor'))
- second_shift_grad: float32 [1024], P(('dp', 'tensor'))
- up_weight_grad: float32 [1024, 4096], P('dp', 'tensor')
- up_bias_grad: float32 [4096], P(('dp', 'tensor'))
- down_weight_grad: float32 [4096, 1024], P('tensor', 'dp')
- down_bias_grad: float32 [1024], P(('dp', 'tensor'))
Inputs may be any that keep to these rules, and one draw needn't show every extreme that they name: lengths holds the number of valid slots of each image, counted from its first slot; slots from there on are padding.
All inputs are finite; a program needn't handle non-finite values.
Results may differ from a plain program's by a relative error of at most 0.017.
Values may be sent and summed in bfloat16 or wider, within the bound.
A program may use at most 192 MiB of HBM per device.

v0:
```python
import jax
import jax.numpy as jnp
from jax import lax
from jax.sharding import PartitionSpec as P

HEAD_DIM = 64
MICRO = 2


EPSILON = 1e-06


def norm_rows(values, gain, shift):
    average = jnp.mean(values, axis=-1, keepdims=True)
    centered = values - average
    variance = jnp.mean(centered * centered, axis=-1, keepdims=True)
    return centered * lax.rsqrt(variance + EPSILON) * gain + shift


def exact_gelu(values):
    return jax.nn.gelu(values, approximate=False)


def spread_rows(local_rows):
    return lax.all_gather(local_rows, "tensor", axis=0, tiled=True)


def fold_rows(partial_rows):
    return lax.psum_scatter(
        partial_rows.astype(jnp.bfloat16), "tensor", scatter_dimension=0, tiled=True
    ).astype(jnp.float32)


def spread_grads(local_rows):
    return lax.all_gather(local_rows, "tensor", axis=0, tiled=True)


def fold_grads(partial_rows):
    return lax.psum_scatter(
        partial_rows.astype(jnp.bfloat16), "tensor", scatter_dimension=0, tiled=True
    ).astype(jnp.float32)


def fetch_weights(qkv_weight, out_weight, up_weight, down_weight):
    return (
        lax.all_gather(qkv_weight, "dp", axis=1, tiled=True),
        lax.all_gather(out_weight, "dp", axis=1, tiled=True),
        lax.all_gather(up_weight, "dp", axis=0, tiled=True),
        lax.all_gather(down_weight, "dp", axis=1, tiled=True),
    )


def head_split(rows, heads_here):
    return rows.reshape(rows.shape[0], rows.shape[1], heads_here, rows.shape[2] // heads_here)


def masked_scores(query_heads, key_heads, key_valid, score_scale):
    scores = (
        jnp.einsum("bqhc,bkhc->bhqk", query_heads, key_heads, preferred_element_type=jnp.float32)
        * score_scale
    )
    return jnp.where(key_valid[:, None, None, :], scores, -1000000000.0)


def row_total(values):
    return jnp.sum(values, axis=(0, 1), dtype=jnp.float32)


def shards(
    inputs,
    lengths,
    cotangent,
    first_gain,
    first_shift,
    qkv_weight,
    query_bias,
    value_bias,
    out_weight,
    out_bias,
    second_gain,
    second_shift,
    up_weight,
    up_bias,
    down_weight,
    down_bias,
):
    image_count, slot_count, model_width = inputs.shape
    per_micro = image_count // MICRO
    tensor_count = lax.axis_size("tensor")
    tensor_rank = lax.axis_index("tensor")
    local_width = qkv_weight.shape[2]
    local_hidden = up_weight.shape[1]
    heads_here = local_width // HEAD_DIM
    score_scale = HEAD_DIM ** (-0.5)
    bf16 = jnp.bfloat16
    f32 = jnp.float32
    gathered = (
        lax.all_gather(first_gain, ("dp", "tensor"), axis=0, tiled=True),
        lax.all_gather(first_shift, ("dp", "tensor"), axis=0, tiled=True),
        lax.all_gather(query_bias, ("dp", "tensor"), axis=0, tiled=True),
        lax.all_gather(value_bias, ("dp", "tensor"), axis=0, tiled=True),
        lax.all_gather(out_bias, ("dp", "tensor"), axis=0, tiled=True),
        lax.all_gather(second_gain, ("dp", "tensor"), axis=0, tiled=True),
        lax.all_gather(second_shift, ("dp", "tensor"), axis=0, tiled=True),
        lax.all_gather(up_bias, ("dp", "tensor"), axis=0, tiled=True),
        lax.all_gather(down_bias, ("dp", "tensor"), axis=0, tiled=True),
    )
    (
        gain_one,
        shift_one,
        qbias_full,
        vbias_full,
        obias_full,
        gain_two,
        shift_two,
        ubias_full,
        dbias_full,
    ) = tuple((member.astype(f32) for member in gathered))
    query_shift = lax.dynamic_slice_in_dim(qbias_full, tensor_rank * local_width, local_width)
    value_shift = lax.dynamic_slice_in_dim(vbias_full, tensor_rank * local_width, local_width)
    up_shift = lax.dynamic_slice_in_dim(ubias_full, tensor_rank * local_hidden, local_hidden)
    positions = jnp.arange(slot_count, dtype=jnp.int32)
    own_lengths = lax.dynamic_slice_in_dim(lengths, tensor_rank * image_count, image_count)
    own_valid = positions[None, :] < own_lengths[:, None]
    weight_totals = tuple(
        (
            jnp.zeros(member.shape, f32)
            for member in (qkv_weight, out_weight, up_weight, down_weight)
        )
    )
    vector_totals = (
        jnp.zeros((model_width,), f32),
        jnp.zeros((model_width,), f32),
        jnp.zeros((local_width,), f32),
        jnp.zeros((local_width,), f32),
        jnp.zeros((model_width,), f32),
        jnp.zeros((model_width,), f32),
        jnp.zeros((model_width,), f32),
        jnp.zeros((local_hidden,), f32),
        jnp.zeros((model_width,), f32),
    )
    outputs = []
    input_terms = []
    for micro_index in range(MICRO):
        offset = micro_index * per_micro
        qkv_full, out_local, up_local, down_local = fetch_weights(
            qkv_weight, out_weight, up_weight, down_weight
        )
        valid_rows = own_valid[offset : offset + per_micro].astype(f32)[:, :, None]
        masked = inputs[offset : offset + per_micro].astype(f32) * valid_rows
        first_all = spread_rows(norm_rows(masked, gain_one, shift_one).astype(bf16))
        key_lengths = jnp.concatenate(
            [
                lengths[
                    peer_rank * image_count + offset : peer_rank * image_count + offset + per_micro
                ]
                for peer_rank in range(tensor_count)
            ]
        )
        key_valid = positions[None, :] < key_lengths[:, None]
        projected = jnp.einsum("bsd,tde->tbse", first_all, qkv_full, preferred_element_type=f32)
        query_heads = head_split((projected[0] + query_shift).astype(bf16), heads_here)
        key_heads = head_split(projected[1].astype(bf16), heads_here)
        value_heads = head_split((projected[2] + value_shift).astype(bf16), heads_here)
        group_count = first_all.shape[0]
        scores = masked_scores(query_heads, key_heads, key_valid, score_scale)
        highest = jnp.max(scores, axis=-1, keepdims=True)
        shifted = jnp.exp(scores - highest)
        sum_exp = jnp.sum(shifted, axis=-1, keepdims=True)
        log_total = highest + jnp.log(sum_exp)
        weights_low = (shifted / sum_exp).astype(bf16)
        mixed = jnp.einsum("bhqk,bkhc->bqhc", weights_low, value_heads, preferred_element_type=f32)
        mixed = mixed.reshape(group_count, slot_count, local_width).astype(bf16)
        attn_part = jnp.einsum("bsc,ce->bse", mixed, out_local, preferred_element_type=f32)
        middle = masked + fold_rows(attn_part) + obias_full
        second_all = spread_rows(norm_rows(middle, gain_two, shift_two).astype(bf16))
        hidden = (
            jnp.einsum("bsd,df->bsf", second_all, up_local, preferred_element_type=f32) + up_shift
        )
        active = exact_gelu(hidden).astype(bf16)
        mlp_part = jnp.einsum("bsf,fe->bse", active, down_local, preferred_element_type=f32)
        outputs.append((middle + fold_rows(mlp_part) + dbias_full).astype(bf16))
        qkv_full, out_local, up_local, down_local = (
            lax.all_gather(qkv_weight, "dp", axis=1, tiled=True),
            lax.all_gather(out_weight, "dp", axis=1, tiled=True),
            lax.all_gather(up_weight, "dp", axis=0, tiled=True),
            lax.all_gather(down_weight, "dp", axis=1, tiled=True),
        )
        grad_out = cotangent[offset : offset + per_micro].astype(f32)
        grad_mlp_low = grad_out.astype(bf16)
        grad_mlp_all = spread_grads(grad_mlp_low)
        grad_active = jnp.einsum(
            "bse,fe->bsf", grad_mlp_all, down_local, preferred_element_type=f32
        )
        gelu_pull = jax.vjp(exact_gelu, hidden)[1]
        grad_hidden = gelu_pull(grad_active)[0].astype(bf16)
        grad_second = fold_grads(
            jnp.einsum("bsf,df->bsd", grad_hidden, up_local, preferred_element_type=f32)
        )
        second_pull = jax.vjp(norm_rows, middle, gain_two, shift_two)[1]
        grad_mid, grad_gain_two, grad_shift_two = second_pull(grad_second)
        grad_middle = grad_out + grad_mid
        grad_attn_low = grad_middle.astype(bf16)
        grad_attn_all = spread_grads(grad_attn_low)
        grad_mixed = jnp.einsum(
            "bse,ce->bsc", grad_attn_all, out_local, preferred_element_type=f32
        ).astype(bf16)
        grad_heads = head_split(grad_mixed, heads_here)
        scores = masked_scores(query_heads, key_heads, key_valid, score_scale)
        probs = jnp.exp(scores - log_total)
        grad_weights = jnp.einsum(
            "bqhc,bkhc->bhqk", grad_heads, value_heads, preferred_element_type=f32
        )
        value_grad = jnp.einsum(
            "bhqk,bqhc->bkhc", probs.astype(bf16), grad_heads, preferred_element_type=f32
        ).astype(bf16)
        inner_sum = jnp.sum(probs * grad_weights, axis=-1, keepdims=True)
        grad_scores = (probs * (grad_weights - inner_sum)).astype(bf16)
        query_grad = (
            jnp.einsum("bhqk,bkhc->bqhc", grad_scores, key_heads, preferred_element_type=f32)
            * score_scale
        ).astype(bf16)
        key_grad = (
            jnp.einsum("bhqk,bqhc->bkhc", grad_scores, query_heads, preferred_element_type=f32)
            * score_scale
        ).astype(bf16)
        grad_project = jnp.stack([query_grad, key_grad, value_grad]).reshape(
            3, group_count, slot_count, local_width
        )
        grad_first = fold_grads(
            jnp.einsum("tbse,tde->bsd", grad_project, qkv_full, preferred_element_type=f32)
        )
        first_pull = jax.vjp(norm_rows, masked, gain_one, shift_one)[1]
        grad_in, grad_gain_one, grad_shift_one = first_pull(grad_first)
        input_terms.append((grad_middle + grad_in) * valid_rows)
        micro_grads = (
            jnp.einsum("bsd,tbse->tde", first_all, grad_project, preferred_element_type=f32),
            jnp.einsum("bsc,bse->ce", mixed, grad_attn_all, preferred_element_type=f32),
            jnp.einsum("bsd,bsf->df", second_all, grad_hidden, preferred_element_type=f32),
            jnp.einsum("bsf,bse->fe", active, grad_mlp_all, preferred_element_type=f32),
        )
        shares = (
            lax.psum_scatter(micro_grads[0], "dp", scatter_dimension=1, tiled=True),
            lax.psum_scatter(micro_grads[1], "dp", scatter_dimension=1, tiled=True),
            lax.psum_scatter(micro_grads[2], "dp", scatter_dimension=0, tiled=True),
            lax.psum_scatter(micro_grads[3], "dp", scatter_dimension=1, tiled=True),
        )
        weight_totals = tuple((total + share for total, share in zip(weight_totals, shares)))
        vector_terms = (
            grad_gain_one,
            grad_shift_one,
            row_total(grad_project[0]),
            row_total(grad_project[2]),
            row_total(grad_attn_low),
            grad_gain_two,
            grad_shift_two,
            row_total(grad_hidden),
            row_total(grad_mlp_low),
        )
        vector_totals = tuple((total + term for total, term in zip(vector_totals, vector_terms)))
    zeros_width = jnp.zeros((model_width,), f32)
    query_full = lax.dynamic_update_slice_in_dim(
        zeros_width, vector_totals[2], tensor_rank * local_width, 0
    )
    value_full = lax.dynamic_update_slice_in_dim(
        zeros_width, vector_totals[3], tensor_rank * local_width, 0
    )
    hidden_full = lax.dynamic_update_slice_in_dim(
        jnp.zeros((local_hidden * tensor_count,), f32),
        vector_totals[7],
        tensor_rank * local_hidden,
        0,
    )
    vector_shares = (
        lax.psum_scatter(vector_totals[0], ("dp", "tensor"), scatter_dimension=0, tiled=True),
        lax.psum_scatter(vector_totals[1], ("dp", "tensor"), scatter_dimension=0, tiled=True),
        lax.psum_scatter(query_full, ("dp", "tensor"), scatter_dimension=0, tiled=True),
        lax.psum_scatter(value_full, ("dp", "tensor"), scatter_dimension=0, tiled=True),
        lax.psum_scatter(vector_totals[4], ("dp", "tensor"), scatter_dimension=0, tiled=True),
        lax.psum_scatter(vector_totals[5], ("dp", "tensor"), scatter_dimension=0, tiled=True),
        lax.psum_scatter(vector_totals[6], ("dp", "tensor"), scatter_dimension=0, tiled=True),
        lax.psum_scatter(hidden_full, ("dp", "tensor"), scatter_dimension=0, tiled=True),
        lax.psum_scatter(vector_totals[8], ("dp", "tensor"), scatter_dimension=0, tiled=True),
    )
    output = jnp.concatenate(outputs, axis=0)
    input_grad = jnp.concatenate(input_terms, axis=0)
    return (
        output,
        input_grad,
        vector_shares[0],
        vector_shares[1],
        weight_totals[0],
        vector_shares[2],
        vector_shares[3],
        weight_totals[1],
        vector_shares[4],
        vector_shares[5],
        vector_shares[6],
        weight_totals[2],
        vector_shares[7],
        weight_totals[3],
        vector_shares[8],
    )


def solution(mesh):
    placed = (
        P(("dp", "tensor"), None, None),
        P("dp"),
        P(("dp", "tensor"), None, None),
        P(("dp", "tensor")),
        P(("dp", "tensor")),
        P(None, "dp", "tensor"),
        P(("dp", "tensor")),
        P(("dp", "tensor")),
        P("tensor", "dp"),
        P(("dp", "tensor")),
        P(("dp", "tensor")),
        P(("dp", "tensor")),
        P("dp", "tensor"),
        P(("dp", "tensor")),
        P("tensor", "dp"),
        P(("dp", "tensor")),
    )
    return jax.shard_map(
        shards,
        mesh=mesh,
        in_specs=placed,
        out_specs=(
            P(("dp", "tensor"), None, None),
            P(("dp", "tensor"), None, None),
            P(("dp", "tensor")),
            P(("dp", "tensor")),
            P(None, "dp", "tensor"),
            P(("dp", "tensor")),
            P(("dp", "tensor")),
            P("tensor", "dp"),
            P(("dp", "tensor")),
            P(("dp", "tensor")),
            P(("dp", "tensor")),
            P("dp", "tensor"),
            P(("dp", "tensor")),
            P("tensor", "dp"),
            P(("dp", "tensor")),
        ),
        check_vma=False,
    )
```

profile of v0, /device:TPU:0, one launch (start us, length us, event | category | flops | bytes accessed | tf_op | source)
XLA Modules:
  0.0 1146.3 jit_solution(12303236237912511767)
XLA Ops:
  13.1 42.2 %all-reduce.19 = (bf16[1024]{0:T(1024)(128)(2,1)S(1)}, bf16[1024]{0:T(1024)(128)(2,1)S(1)}, bf16[1024]{0:T(1024)(128)(2,1)}, bf16[1024]{0:T(1024)(128)(2,1)S(1)}...) all-reduce(bf16[1024]{0:T(1024)(128)(2,1)S(1)} %dynamic-update-slic, ...), channel_id=1, replica_groups=mesh['dp'=16,'tensor'=2] {'dp','tensor'}, use_global_device_ids=true, to_apply=%add.2 | all-reduce | flops 8192 | bytes 32768
  64.8 17.6 %all-gather.26.cloned.1.call-done = bf16[2,320,1024]{2,1,0:T(8,128)(2,1)} async-done(((bf16[1,320,1024]{2,1,0:T(8,128)(2,1)}), bf16[2,320,1024]{2,1,0:T(8,128)(2,1)}) %all-gather.26.cloned.1.call-update) | async-done | bytes 1310736 | tf_op jit(solution)/shard_map/all_gather | solution.py:25
  82.3 47.7 %all-gather.16.cloned.1.call-done = bf16[3,1024,512]{2,1,0:T(8,128)(2,1)} async-done(((bf16[3,64,512]{2,1,0:T(8,128)(2,1)}), bf16[3,1024,512]{2,1,0:T(8,128)(2,1)}) %all-gather.16.cloned.1.call-update) | async-done | bytes 3145744 | tf_op jit(solution)/shard_map/all_gather | solution.py:46
  130.1 4.5 fusion.58
  139.7 7.0 fusion.42
  146.7 8.1 all-gather.14.cloned.1.call-done
  154.8 4.5 fusion.55
  162.9 4.9 fusion.1
  168.4 6.4 fusion.85
  174.8 19.9 %all-gather.18.cloned.1.call-done = bf16[512,1024]{0,1:T(8,128)(2,1)} async-done(((bf16[512,64]{0,1:T(8,128)(2,1)}), bf16[512,1024]{0,1:T(8,128)(2,1)}) %all-gather.18.cloned.1.call-update) | async-done | bytes 1048592 | tf_op jit(solution)/shard_map/all_gather | solution.py:47
  220.9 26.0 %reduce-scatter.12.cloned.1.call-done = bf16[1,320,1024]{2,1,0:T(8,128)(2,1)} async-done(((bf16[2,320,1024]{2,1,0:T(8,128)(2,1)}), bf16[1,320,1024]{2,1,0:T(8,128)(2,1)}) %reduce-scatter.12.cloned.1.call-update) | async-done | bytes 655376 | tf_op jit(solution)/shard_map/reduce_scatter | solution.py:29
  256.4 67.7 %all-gather = bf16[32,1,128]{2,1,0:T(2,128)(2,1)S(1)} all-gather(bf16[1,1,128]{2,1,0:T(2,128)(2,1)S(1)} %bitcast.210), channel_id=1, replica_groups=mesh['dp'=16,'tensor'=2] {'dp','tensor'}, dimensions={0}, use_global_device_ids=true | all-gather | bytes 8448 | tf_op jit(solution)/shard_map/all_gather | solution.py:105
  324.6 7.8 fusion.29
  332.5 18.5 %all-gather.20.cloned.1.call-done = bf16[2,320,1024]{2,1,0:T(8,128)(2,1)} async-done(((bf16[1,320,1024]{2,1,0:T(8,128)(2,1)}), bf16[2,320,1024]{2,1,0:T(8,128)(2,1)}) %all-gather.20.cloned.1.call-update) | async-done | bytes 1310736 | tf_op jit(solution)/shard_map/all_gather | solution.py:25
  351.0 10.7 fusion.114
  364.0 26.5 %multiply_convert_fusion.3 = (bf16[2,320,2048]{2,1,0:T(8,128)(2,1)}, f32[2,320,2048]{2,1,0:T(8,128)}, bf16[2,320,2048]{2,1,0:T(8,128)(2,1)}, f32[2,320,2048]{2,1,0:T(8,128)}) fusion(f32[2,320,2048]{2,1,0:T(8,128)S(1)} %get-tuple-element.151, f32[2048]{0:T(1024)S(1)} %dynamic_slice.15, u8[320,2048]{1,0:T(8,128)(4,1)S(1)} %get-tuple-element.61, ...), kind=kLoop, calls=%fused_computation.50 | loop fusion | flops 184811520 | bytes 28844032 | tf_op jit(solution)/shard_map/convert_element_type | solution.py:180
  390.5 38.7 %all-gather.24.cloned.1.call-done = bf16[2048,1024]{0,1:T(8,128)(2,1)} async-done(((bf16[2048,64]{0,1:T(8,128)(2,1)}), bf16[2048,1024]{0,1:T(8,128)(2,1)}) %all-gather.24.cloned.1.call-update) | async-done | bytes 4194320 | tf_op jit(solution)/shard_map/all_gather | solution.py:49
  429.2 10.9 convert_reduce_fusion
  441.6 4.0 fusion.68
  445.9 7.5 all-gather.30.cloned.1.call-done
  453.4 10.9 convert_reduce_fusion.1
  465.9 4.0 fusion.65
  469.9 7.0 fusion.71
  477.0 7.0 fusion.74
  484.6 20.4 %reduce-scatter.20.cloned.1.call-done = bf16[1,320,1024]{2,1,0:T(8,128)(2,1)} async-done(((bf16[2,320,1024]{2,1,0:T(8,128)(2,1)}), bf16[1,320,1024]{2,1,0:T(8,128)(2,1)}) %reduce-scatter.20.cloned.1.call-update) | async-done | bytes 655376 | tf_op jit(solution)/shard_map/reduce_scatter | solution.py:39
  508.4 21.9 %reduce-scatter.14.cloned.1.call-done = bf16[1,320,1024]{2,1,0:T(8,128)(2,1)} async-done(((bf16[2,320,1024]{2,1,0:T(8,128)(2,1)}), bf16[1,320,1024]{2,1,0:T(8,128)(2,1)}) %reduce-scatter.14.cloned.1.call-update) | async-done | bytes 655376 | tf_op jit(solution)/shard_map/reduce_scatter | solution.py:29
  533.6 22.1 %reduce-scatter.18.cloned.1.call-done = bf16[1,320,1024]{2,1,0:T(8,128)(2,1)} async-done(((bf16[2,320,1024]{2,1,0:T(8,128)(2,1)}), bf16[1,320,1024]{2,1,0:T(8,128)(2,1)}) %reduce-scatter.18.cloned.1.call-update) | async-done | bytes 655376 | tf_op jit(solution)/shard_map/reduce_scatter | solution.py:29
  562.6 23.0 %all-gather.32.cloned.1.call-done = bf16[2,320,1024]{2,1,0:T(8,128)(2,1)} async-done(((bf16[1,320,1024]{2,1,0:T(8,128)(2,1)}), bf16[2,320,1024]{2,1,0:T(8,128)(2,1)}) %all-gather.32.cloned.1.call-update) | async-done | bytes 1310736 | tf_op jit(solution)/shard_map/all_gather | solution.py:35
  589.2 7.2 multiply_reduce_fusion.1
  603.0 4.4 multiply_convert_fusion.6
  609.6 6.1 convert_reduce_fusion.9
  620.5 5.7 bitcast_convert_fusion.1
  626.4 7.2 multiply_reduce_fusion
  640.9 4.3 multiply_convert_fusion.4
  647.4 5.6 convert_reduce_fusion.8
  654.2 5.9 bitcast_convert_fusion
  660.2 4.1 fusion.103
  664.4 4.6 fusion.2
  668.9 9.5 copy.117
  684.1 5.8 fusion.159
  690.0 6.0 bitcast_add_fusion.1
  696.2 5.8 fusion.160
  702.1 6.0 bitcast_add_fusion
  716.0 41.7 %all-reduce.18 = (f32[1024]{0:T(1024)S(1)}, f32[1024]{0:T(1024)S(1)}, f32[1024]{0:T(1024)S(1)}, f32[1024]{0:T(1024)S(1)}, f32[1024]{0:T(1024)S(1)}, /*index=5*/f...) all-reduce(f32[1024]{0:T(1024)S(1)} %add.342, ...), channel_id=14, replica_groups=mesh['dp'=16,'tensor'=2] {'dp','tensor'}, use_global_device_ids=true, to_apply=%region_32.33.clone | all-reduce | flops 12288 | bytes 98304
  767.6 90.9 %all-reduce.22.cloned.1.call-done = f32[3,1024,512]{2,0,1:T(4,128)} async-done(((f32[3,1024,512]{2,0,1:T(4,128)}), f32[3,1024,512]{2,0,1:T(4,128)}) %all-reduce.22.cloned.1.call-update) | async-done | bytes 6291472
  860.5 64.0 %reduce-scatter.28.cloned.1.call-done = f32[512,64]{0,1:T(8,128)} async-done(((f32[512,1024]{0,1:T(8,128)}), f32[512,64]{0,1:T(8,128)}) %reduce-scatter.28.cloned.1.call-update) | async-done | bytes 131088 | tf_op jit(solution)/shard_map/reduce_scatter | solution.py:244
  924.5 107.1 %reduce-scatter.30.cloned.1.call-done = f32[64,2048]{1,0:T(8,128)} async-done(((f32[1024,2048]{1,0:T(8,128)}), f32[64,2048]{1,0:T(8,128)}) %reduce-scatter.30.cloned.1.call-update) | async-done | bytes 524304 | tf_op jit(solution)/shard_map/reduce_scatter | solution.py:245
  1031.6 107.6 %reduce-scatter.32.cloned.1.call-done = f32[2048,64]{0,1:T(8,128)} async-done(((f32[2048,1024]{0,1:T(8,128)}), f32[2048,64]{0,1:T(8,128)}) %reduce-scatter.32.cloned.1.call-update) | async-done | bytes 524304 | tf_op jit(solution)/shard_map/reduce_scatter | solution.py:246
  (402 shorter events, 132.4 us)
Async XLA Ops:
  7.3 75.1 %all-gather.26.cloned.1.call-start = ((), (), s32[]{:S(2)}) async-start(), calls=%async_computation.19 | async-start | bytes 1966080 | tf_op jit(solution)/shard_map/all_gather | solution.py:25
  9.9 47.6 %copy-start.51 = (f32[320]{0:T(512)}, f32[320]{0:T(512)S(1)}, u32[]{:S(2)}) copy-start(f32[320]{0:T(512)S(1)} %get-tuple-element.170) | copy-start | bytes 3844
  10.0 47.6 %copy-start.53 = (f32[320]{0:T(512)}, f32[320]{0:T(512)S(1)}, u32[]{:S(2)}) copy-start(f32[320]{0:T(512)S(1)} %get-tuple-element.171) | copy-start | bytes 3844
  10.6 48.5 %copy-start.65 = (f32[320]{0:T(512)}, f32[320]{0:T(512)S(1)}, u32[]{:S(2)}) copy-start(f32[320]{0:T(512)S(1)} %get-tuple-element.85) | copy-start | bytes 3844
  11.1 47.9 %copy-start.57 = (f32[320]{0:T(512)}, f32[320]{0:T(512)S(1)}, u32[]{:S(2)}) copy-start(f32[320]{0:T(512)S(1)} %fusion.128) | copy-start | bytes 3844
  11.1 47.9 %copy-start.55 = (f32[320]{0:T(512)}, f32[320]{0:T(512)S(1)}, u32[]{:S(2)}) copy-start(f32[320]{0:T(512)S(1)} %fusion.130) | copy-start | bytes 3844
  57.6 72.5 %all-gather.16.cloned.1.call-start = ((), (), s32[]{:S(2)}) async-start(), calls=%async_computation.12 | async-start | bytes 3342336 | tf_op jit(solution)/shard_map/all_gather | solution.py:46
  58.3 96.5 %all-gather.14.cloned.1.call-start = ((), (), s32[]{:S(2)}) async-start(), calls=%async_computation.11 | async-start | bytes 1966080 | tf_op jit(solution)/shard_map/all_gather | solution.py:25
  59.1 135.6 %all-gather.18.cloned.1.call-start = ((), (), s32[]{:S(2)}) async-start(), calls=%async_computation.13 | async-start | bytes 1114112 | tf_op jit(solution)/shard_map/all_gather | solution.py:47
  59.7 161.2 %reduce-scatter.16.cloned.1.call-start = ((), (), s32[]{:S(2)}) async-start(), calls=%async_computation.20 | async-start | bytes 1966080 | tf_op jit(solution)/shard_map/reduce_scatter | solution.py:29
  138.3 8.4 copy-start.7
  198.5 48.4 %reduce-scatter.12.cloned.1.call-start = ((), (), s32[]{:S(2)}) async-start(), calls=%async_computation.14 | async-start | bytes 1966080 | tf_op jit(solution)/shard_map/reduce_scatter | solution.py:29
  217.1 107.1 %all-gather.22.cloned.1.call-start = ((), (), s32[]{:S(2)}) async-start(), calls=%async_computation.16 | async-start | bytes 4456448 | tf_op jit(solution)/shard_map/all_gather | solution.py:48
  217.8 106.8 %all-gather.28.cloned.1.call-start = ((), (), s32[]{:S(2)}) async-start(), calls=%async_computation.21 | async-start | bytes 1966080 | tf_op jit(solution)/shard_map/all_gather | solution.py:25
  220.9 28.0 %copy-start.4 = (bf16[1,320,1024]{2,1,0:T(8,128)(2,1)S(1)}, bf16[1,320,1024]{2,1,0:T(8,128)(2,1)}, u32[]{:S(2)}) copy-start(bf16[1,320,1024]{2,1,0:T(8,128)(2,1)} %reduce-scatter.16.cloned.1.call-done) | copy-start | bytes 1966084
  251.8 99.2 %all-gather.20.cloned.1.call-start = ((), (), s32[]{:S(2)}) async-start(), calls=%async_computation.15 | async-start | bytes 1966080 | tf_op jit(solution)/shard_map/all_gather | solution.py:25
  252.6 138.0 %all-gather.34.cloned.1.call-start = ((), (), s32[]{:S(2)}) async-start(), calls=%async_computation.27 | async-start | bytes 1966080 | tf_op jit(solution)/shard_map/all_gather | solution.py:35
  255.1 174.1 %all-gather.24.cloned.1.call-start = ((), (), s32[]{:S(2)}) async-start(), calls=%async_computation.17 | async-start | bytes 4456448 | tf_op jit(solution)/shard_map/all_gather | solution.py:49
  255.8 197.6 %all-gather.30.cloned.1.call-start = ((), (), s32[]{:S(2)}) async-start(), calls=%async_computation.23 | async-start | bytes 1966080 | tf_op jit(solution)/shard_map/all_gather | solution.py:35
  256.4 228.2 %reduce-scatter.24.cloned.1.call-start = ((), (), s32[]{:S(2)}) async-start(), calls=%async_computation.28 | async-start | bytes 1966080 | tf_op jit(solution)/shard_map/reduce_scatter | solution.py:39
  351.0 13.0 %copy-start.26 = (f32[2,320,2048]{2,1,0:T(8,128)S(1)}, f32[2,320,2048]{2,1,0:T(8,128)}, u32[]{:S(2)}) copy-start(f32[2,320,2048]{2,1,0:T(8,128)} %fusion.29) | copy-start | bytes 15728644
  429.2 12.4 %copy-start.86 = (bf16[1024,2048]{1,0:T(8,128)(2,1)S(1)}, bf16[1024,2048]{1,0:T(8,128)(2,1)}, u32[]{:S(2)}) copy-start(bf16[1024,2048]{1,0:T(8,128)(2,1)} %all-gather.22.cloned.1.call-done) | copy-start | bytes 12582916
  445.7 59.3 %reduce-scatter.20.cloned.1.call-start = ((), (), s32[]{:S(2)}) async-start(), calls=%async_computation.24 | async-start | bytes 1966080 | tf_op jit(solution)/shard_map/reduce_scatter | solution.py:39
  453.4 12.5 %copy-start.87 = (bf16[1024,2048]{1,0:T(8,128)(2,1)S(1)}, bf16[1024,2048]{1,0:T(8,128)(2,1)}, u32[]{:S(2)}) copy-start(bf16[1024,2048]{1,0:T(8,128)(2,1)} %all-gather.22.cloned.1.call-done) | copy-start | bytes 12582916
  469.9 60.5 %reduce-scatter.14.cloned.1.call-start = ((), (), s32[]{:S(2)}) async-start(), calls=%async_computation.18 | async-start | bytes 1966080 | tf_op jit(solution)/shard_map/reduce_scatter | solution.py:29
  477.0 78.8 %reduce-scatter.18.cloned.1.call-start = ((), (), s32[]{:S(2)}) async-start(), calls=%async_computation.22 | async-start | bytes 1966080 | tf_op jit(solution)/shard_map/reduce_scatter | solution.py:29
  477.0 7.5 copy-start.81
  484.1 101.5 %all-gather.32.cloned.1.call-start = ((), (), s32[]{:S(2)}) async-start(), calls=%async_computation.25 | async-start | bytes 1966080 | tf_op jit(solution)/shard_map/all_gather | solution.py:35
  504.9 25.4 %copy-start.29 = (bf16[1,320,1024]{2,1,0:T(8,128)(2,1)S(1)}, bf16[1,320,1024]{2,1,0:T(8,128)(2,1)}, u32[]{:S(2)}) copy-start(bf16[1,320,1024]{2,1,0:T(8,128)(2,1)} %reduce-scatter.20.cloned.1.call-done) | copy-start | bytes 1966084
  533.6 25.3 %copy-start.59 = (f32[320]{0:T(512)}, f32[320]{0:T(512)S(1)}, u32[]{:S(2)}) copy-start(f32[320]{0:T(512)S(1)} %negate_multiply_fusion.5) | copy-start | bytes 3844
  533.6 25.3 %copy-start.11 = (bf16[2,320,1024]{2,1,0:T(8,128)(2,1)S(1)}, bf16[2,320,1024]{2,1,0:T(8,128)(2,1)}, u32[]{:S(2)}) copy-start(bf16[2,320,1024]{2,1,0:T(8,128)(2,1)} %param.18) | copy-start | bytes 3932164
  561.2 55.7 %all-gather.36.cloned.1.call-start = ((), (), s32[]{:S(2)}) async-start(), calls=%async_computation.29 | async-start | bytes 1966080 | tf_op jit(solution)/shard_map/all_gather | solution.py:35
  562.5 26.7 %copy-start.21 = (f32[1,2,320,512]{2,3,1,0:T(8,128)S(1)}, f32[1,2,320,512]{2,3,1,0:T(8,128)}, u32[]{:S(2)}) copy-start(f32[1,2,320,512]{2,3,1,0:T(8,128)} %copy.93) | copy-start | bytes 3932164
  562.5 149.4 %reduce-scatter.22.cloned.1.call-start = ((), (), s32[]{:S(2)}) async-start(), calls=%async_computation.26 | async-start | bytes 1966080 | tf_op jit(solution)/shard_map/reduce_scatter | solution.py:39
  589.2 7.2 slice-start.3
  589.2 7.2 copy-start.41
  589.2 7.2 copy-start.50
  626.3 85.7 %reduce-scatter.26.cloned.1.call-start = ((), (), s32[]{:S(2)}) async-start(), calls=%async_computation.30 | async-start | bytes 1966080 | tf_op jit(solution)/shard_map/reduce_scatter | solution.py:39
  626.3 7.2 slice-start
  626.4 7.2 slice-start.1
  626.4 7.2 copy-start.40
  626.4 7.2 copy-start.47
  660.1 198.5 %all-reduce.22.cloned.1.call-start = ((), (), s32[]{:S(2)}) async-start(), calls=%async_computation.34 | async-start | bytes 16777216
  678.5 246.0 %reduce-scatter.28.cloned.1.call-start = ((), (), s32[]{:S(2)}) async-start(), calls=%async_computation.31 | async-start | bytes 2228224 | tf_op jit(solution)/shard_map/reduce_scatter | solution.py:244
  684.1 347.5 %reduce-scatter.30.cloned.1.call-start = ((), (), s32[]{:S(2)}) async-start(), calls=%async_computation.32 | async-start | bytes 8912896 | tf_op jit(solution)/shard_map/reduce_scatter | solution.py:245
  696.0 443.2 %reduce-scatter.32.cloned.1.call-start = ((), (), s32[]{:S(2)}) async-start(), calls=%async_computation.33 | async-start | bytes 8912896 | tf_op jit(solution)/shard_map/reduce_scatter | solution.py:246
  714.4 48.6 %copy-start.12 = (bf16[2,320,1024]{2,1,0:T(8,128)(2,1)S(1)}, bf16[2,320,1024]{2,1,0:T(8,128)(2,1)}, u32[]{:S(2)}) copy-start(bf16[2,320,1024]{2,1,0:T(8,128)(2,1)} %param.18) | copy-start | bytes 3932164
  714.4 48.6 %copy-start.60 = (f32[320]{0:T(512)S(1)}, f32[320]{0:T(512)}, u32[]{:S(2)}) copy-start(f32[320]{0:T(512)} %copy-done.59) | copy-start | bytes 3844
  (84 other events, 280.8 us)
Sparse Core Ops, SparseCore 0:
  57.7 24.5 all-gather.25
  84.5 45.4 all-gather.15
  132.2 22.5 all-gather.13
  156.8 37.8 all-gather.17
  198.6 22.2 reduce-scatter.15
  223.6 23.2 reduce-scatter.11
  249.1 50.5 all-gather.21
  301.8 22.7 all-gather.27
  326.7 24.1 all-gather.19
  352.4 24.2 all-gather.33
  378.8 50.3 all-gather.23
  430.6 22.7 all-gather.29
  455.6 23.2 reduce-scatter.23
  481.6 23.2 reduce-scatter.19
  507.0 23.2 reduce-scatter.13
  532.4 23.2 reduce-scatter.17
  561.3 24.2 all-gather.31
  587.0 24.2 all-gather.35
  626.4 23.2 reduce-scatter.21
  660.2 23.2 reduce-scatter.25
  687.2 171.2 all-reduce.21
  862.8 61.6 reduce-scatter.27
  929.2 102.3 reduce-scatter.29
  1036.1 103.0 reduce-scatter.31
where the time goes:
time: 1150 us
  waiting for transfers between devices  649 us (56%)
  matrix products  190 us (17%)
  blocking collectives  152 us (13%)
  other arithmetic  74.5 us (6%)
  local copies, waits for them, and re-layouts  61.6 us (5%)
  between operations  16.9 us (1%)
    reduce_scatter x1, waiting for transfers between devices, shards(): lax.psum_scatter(micro_grads[3], 'dp', scatter_dimension=1, tiled=True)  108 us
    reduce_scatter x1, waiting for transfers between devices, shards(): lax.psum_scatter(micro_grads[2], 'dp', scatter_dimension=0, tiled=True)  107 us
    unnamed x25, waiting for transfers between devices  95.6 us
    unnamed x2, blocking collectives  83.9 us
    reduce_scatter x4, waiting for transfers between devices, fold_rows(): lax.psum_scatter(partial_rows.astype(jnp.bfloat16), 'tensor', scatter_dim...  73 us
    all_gather x1, blocking collectives, shards(): lax.all_gather(up_bias, ('dp', 'tensor'), axis=0, tiled=True)  67.7 us
    reduce_scatter x1, waiting for transfers between devices, shards(): lax.psum_scatter(micro_grads[1], 'dp', scatter_dimension=1, tiled=True)  64 us
    all_gather x1, waiting for transfers between devices, fetch_weights(): lax.all_gather(qkv_weight, 'dp', axis=1, tiled=True)  47.7 us
  transfers between devices with their start and end apart: 24, of which 18 were waited for; matrix products, arithmetic and copies ran while one was open for 25% of the time, Pallas kernels for 0%

commit v1 on v0

v1 whole, which is shorter than its diff:
```python
import jax
import jax.numpy as jnp
from jax import lax
from jax.sharding import PartitionSpec as P

HEAD_DIM = 64
EPSILON = 1e-06
BOTH = ("dp", "tensor")
bf16 = jnp.bfloat16
f32 = jnp.float32


def exact_gelu(values):
    return jax.nn.gelu(values, approximate=False)


def norm_stats(values):
    average = jnp.mean(values, axis=-1, keepdims=True)
    centered = values - average
    variance = jnp.mean(centered * centered, axis=-1, keepdims=True)
    scale = lax.rsqrt(variance + EPSILON)
    return centered * scale, scale


def norm_back(grad, unit, scale, gain):
    z = grad * gain
    mean_z = jnp.mean(z, axis=-1, keepdims=True)
    mean_zx = jnp.mean(z * unit, axis=-1, keepdims=True)
    return scale * (z - mean_z - unit * mean_zx)


def gather_matrix(shard):
    wide = lax.all_gather(shard, "tensor", axis=1, tiled=True)
    return lax.all_gather(wide, "dp", axis=0, tiled=True)


def scatter_matrix(grad):
    rows, columns = grad.shape
    halves = jnp.stack(jnp.split(grad, lax.axis_size("tensor"), axis=1))
    halves = halves.reshape(-1, columns // lax.axis_size("tensor"))
    return lax.psum_scatter(halves, ("tensor", "dp"), scatter_dimension=0, tiled=True)


def mm(a, b, dims):
    return lax.dot_general(a, b, (dims, ((), ())), preferred_element_type=f32)


NN = ((1,), (0,))
NT = ((1,), (1,))
TN = ((0,), (0,))


def shards(
    inputs,
    lengths,
    cotangent,
    first_gain,
    first_shift,
    qkv_weight,
    query_bias,
    value_bias,
    out_weight,
    out_bias,
    second_gain,
    second_shift,
    up_weight,
    up_bias,
    down_weight,
    down_bias,
):
    image_count, slot_count, width = inputs.shape
    tensor_rank = lax.axis_index("tensor")
    heads = width // HEAD_DIM
    tokens = image_count * slot_count
    score_scale = HEAD_DIM ** (-0.5)
    device_count = lax.axis_size("dp") * lax.axis_size("tensor")

    vectors = (
        first_gain,
        first_shift,
        query_bias,
        value_bias,
        out_bias,
        second_gain,
        second_shift,
        down_bias,
        up_bias,
    )
    sizes = [v.shape[0] for v in vectors]
    packed = lax.all_gather(jnp.concatenate(vectors), BOTH, axis=0)
    full = []
    start = 0
    for size in sizes:
        full.append(packed[:, start : start + size].reshape(-1).astype(f32))
        start += size
    gain_one, shift_one, qbias, vbias, obias, gain_two, shift_two, dbias, ubias = full

    query_w = gather_matrix(qkv_weight[0])
    key_w = gather_matrix(qkv_weight[1])
    value_w = gather_matrix(qkv_weight[2])
    out_t = gather_matrix(out_weight.T)
    up_w = gather_matrix(up_weight)
    down_t = gather_matrix(down_weight.T)

    positions = jnp.arange(slot_count, dtype=jnp.int32)
    own_lengths = lax.dynamic_slice_in_dim(lengths, tensor_rank * image_count, image_count)
    valid = positions[None, :] < own_lengths[:, None]
    valid_rows = valid.astype(f32).reshape(tokens, 1)
    masked = inputs.reshape(tokens, width).astype(f32) * valid_rows
    unit_one, scale_one = norm_stats(masked)
    first = (unit_one * gain_one + shift_one).astype(bf16)

    def split(rows):
        return rows.reshape(image_count, slot_count, heads, HEAD_DIM)

    query = split((mm(first, query_w, NN) + qbias).astype(bf16))
    key = split(mm(first, key_w, NN).astype(bf16))
    value = split((mm(first, value_w, NN) + vbias).astype(bf16))
    scores = jnp.einsum("bqhc,bkhc->bhqk", query, key, preferred_element_type=f32) * score_scale
    scores = jnp.where(valid[:, None, None, :], scores, -1000000000.0)
    highest = jnp.max(scores, axis=-1, keepdims=True)
    shifted = jnp.exp(scores - highest)
    probs = shifted / jnp.sum(shifted, axis=-1, keepdims=True)
    weights_low = probs.astype(bf16)
    mixed = jnp.einsum("bhqk,bkhc->bqhc", weights_low, value, preferred_element_type=f32)
    mixed = mixed.astype(bf16).reshape(tokens, width)
    middle = masked + mm(mixed, out_t, NT) + obias
    unit_two, scale_two = norm_stats(middle)
    second = (unit_two * gain_two + shift_two).astype(bf16)
    hidden = mm(second, up_w, NN) + ubias
    active = exact_gelu(hidden).astype(bf16)
    output = (middle + mm(active, down_t, NT) + dbias).astype(bf16)

    grad_low = cotangent.reshape(tokens, width)
    grad_out = grad_low.astype(f32)
    down_grad = scatter_matrix(mm(grad_low, active, TN).astype(bf16))
    grad_active = mm(grad_low, down_t, NN)
    grad_hidden32 = jax.vjp(exact_gelu, hidden)[1](grad_active)[0]
    grad_hidden = grad_hidden32.astype(bf16)
    up_grad = scatter_matrix(mm(second, grad_hidden, TN).astype(bf16))
    grad_second = mm(grad_hidden, up_w, NT)
    grad_middle = grad_out + norm_back(grad_second, unit_two, scale_two, gain_two)
    grad_attn = grad_middle.astype(bf16)
    out_grad = scatter_matrix(mm(grad_attn, mixed, TN).astype(bf16))
    grad_mixed = split(mm(grad_attn, out_t, NN).astype(bf16))
    grad_weights = jnp.einsum("bqhc,bkhc->bhqk", grad_mixed, value, preferred_element_type=f32)
    value_grad = jnp.einsum("bhqk,bqhc->bkhc", weights_low, grad_mixed, preferred_element_type=f32)
    value_grad = value_grad.astype(bf16).reshape(tokens, width)
    inner = jnp.sum(probs * grad_weights, axis=-1, keepdims=True)
    grad_scores = (probs * (grad_weights - inner)).astype(bf16)
    query_grad = (
        jnp.einsum("bhqk,bkhc->bqhc", grad_scores, key, preferred_element_type=f32) * score_scale
    )
    key_grad = (
        jnp.einsum("bhqk,bqhc->bkhc", grad_scores, query, preferred_element_type=f32) * score_scale
    )
    query_grad = query_grad.astype(bf16).reshape(tokens, width)
    key_grad = key_grad.astype(bf16).reshape(tokens, width)
    qkv_grad = jnp.stack(
        [
            scatter_matrix(mm(first, query_grad, TN).astype(bf16)),
            scatter_matrix(mm(first, key_grad, TN).astype(bf16)),
            scatter_matrix(mm(first, value_grad, TN).astype(bf16)),
        ]
    )
    grad_first = mm(query_grad, query_w, NT) + mm(key_grad, key_w, NT) + mm(value_grad, value_w, NT)
    grad_in = norm_back(grad_first, unit_one, scale_one, gain_one)
    input_grad = (grad_middle + grad_in) * valid_rows

    def total(values):
        return jnp.sum(values.astype(f32), axis=0)

    vector_grads = (
        total(grad_first * unit_one),
        total(grad_first),
        total(query_grad),
        total(value_grad),
        total(grad_attn),
        total(grad_second * unit_two),
        total(grad_second),
        total(grad_low),
        total(grad_hidden),
    )
    stacked = jnp.concatenate([v.reshape(device_count, -1) for v in vector_grads], axis=1)
    own = lax.psum_scatter(stacked, BOTH, scatter_dimension=0, tiled=True)[0]
    shares = []
    start = 0
    for size in sizes:
        shares.append(own[start : start + size])
        start += size

    return (
        output.reshape(inputs.shape),
        input_grad.reshape(inputs.shape),
        shares[0],
        shares[1],
        qkv_grad.astype(f32),
        shares[2],
        shares[3],
        out_grad.T.astype(f32),
        shares[4],
        shares[5],
        shares[6],
        up_grad.astype(f32),
        shares[8],
        down_grad.T.astype(f32),
        shares[7],
    )


def solution(mesh):
    rows = P(BOTH, None, None)
    vector = P(BOTH)
    return jax.shard_map(
        shards,
        mesh=mesh,
        in_specs=(
            rows,
            P("dp"),
            rows,
            vector,
            vector,
            P(None, "dp", "tensor"),
            vector,
            vector,
            P("tensor", "dp"),
            vector,
            vector,
            vector,
            P("dp", "tensor"),
            vector,
            P("tensor", "dp"),
            vector,
        ),
        out_specs=(
            rows,
            rows,
            vector,
            vector,
            P(None, "dp", "tensor"),
            vector,
            vector,
            P("tensor", "dp"),
            vector,
            vector,
            vector,
            P("dp", "tensor"),
            vector,
            P("tensor", "dp"),
            vector,
        ),
        check_vma=False,
    )
```

time: 1150 us -> 1270 us (1.10)
  waiting for transfers between devices: 649 us -> 798 us
  other arithmetic: 74.5 us -> 55.1 us
  matrix products: 190 us -> 174 us
  local copies, waits for them, and re-layouts: 61.6 us -> 77 us
    reduce_scatter x11 -> x6, waiting for transfers between devices: 372 us -> 664 us  [scatter_matrix(): lax.psum_scatter(halves, ('tensor', 'dp'), scatter_dimension=0, tiled=True)]
    unnamed x25 -> x12, waiting for transfers between devices: 95.6 us -> 0.2 us
    reshape x0 -> x20, local copies, waits for them, and re-layouts: none -> 53.2 us  [the longest x8 37 us: split(): return rows.reshape(image_count, slot_count, heads, HEAD_DIM)]
    all_gather x12 -> x6, waiting for transfers between devices: 181 us -> 133 us  [gather_matrix(): return lax.all_gather(wide, 'dp', axis=0, tiled=True)]
    unnamed x2 -> x1, blocking collectives: 83.9 us -> 39.7 us
    all_gather x1 -> x7, blocking collectives: 67.7 us -> 106 us  [the longest x1 65.8 us: shards(): packed = lax.all_gather(jnp.concatenate(vectors), BOTH, axis=0)]
    dot_general x36 -> x23, matrix products: 190 us -> 163 us  [the longest x18 125 us: mm(): return lax.dot_general(a, b, (dims, ((), ())), preferred_element_type=f32)]
    reduce_sum x12 -> x5, other arithmetic: 27.9 us -> 2.77 us  [the longest x2 1.38 us: total(): return jnp.sum(values.astype(f32), axis=0)]
  transfers between devices with their start and end apart: 24 -> 12, of which waited for: 18 -> 8; matrix products, arithmetic and copies ran while one was open for 25% -> 18% of each run, Pallas kernels for 0% -> 0%
where the time goes in v1:
time: 1270 us
  waiting for transfers between devices  798 us (63%)
  matrix products  174 us (14%)
  blocking collectives  146 us (11%)
  local copies, waits for them, and re-layouts  77 us (6%)
  other arithmetic  55.1 us (4%)
  between operations  15.1 us (1%)
    reduce_scatter x6, waiting for transfers between devices, scatter_matrix(): lax.psum_scatter(halves, ('tensor', 'dp'), scatter_dimension=0, tiled=True)  664 us
    all_gather x6, waiting for transfers between devices, gather_matrix(): return lax.all_gather(wide, 'dp', axis=0, tiled=True)  133 us
    dot_general x18, matrix products, mm(): return lax.dot_general(a, b, (dims, ((), ())), preferred_element_type=f32)  125 us
    all_gather x1, blocking collectives, shards(): packed = lax.all_gather(jnp.concatenate(vectors), BOTH, axis=0)  65.8 us
    all_gather x6, blocking collectives, gather_matrix(): wide = lax.all_gather(shard, 'tensor', axis=1, tiled=True)  40.1 us
    unnamed x1, blocking collectives  39.7 us
    reshape x8, local copies, waits for them, and re-layouts, split(): return rows.reshape(image_count, slot_count, heads, HEAD_DIM)  37 us
  transfers between devices with their start and end apart: 12, of which 8 were waited for; matrix products, arithmetic and copies ran while one was open for 18% of the time, Pallas kernels for 0%

profile of v1, /device:TPU:0, one launch (start us, length us, event | category | flops | bytes accessed | tf_op | source)
XLA Modules:
  0.0 1265.2 jit_solution(6776043386296748097)
XLA Ops:
  8.4 6.0 all-gather.5
  14.5 5.0 all-gather.1
  19.6 5.0 all-gather.3
  24.7 7.3 all_gather.50
  32.1 9.3 all_gather.52
  41.5 7.3 all_gather.54
  50.6 65.8 %all-gather.7 = bf16[32,1,384]{2,1,0:T(2,128)(2,1)S(1)} all-gather(bf16[1,1,384]{2,1,0:T(2,128)(2,1)S(1)} %reshape.425), channel_id=2, replica_groups=mesh['dp'=16,'tensor'=2] {'dp','tensor'}, dimensions={0}, use_global_device_ids=true | all-gather | bytes 25344 | tf_op jit(solution)/shard_map/all_gather | solution.py:90
  120.0 4.6 fusion.35
  124.6 5.0 reshape.430
  129.6 3.9 copy.67
  133.6 5.2 add_convert_fusion.5
  138.8 4.4 reshape.428
  143.3 4.8 copy.68
  148.0 4.7 add_convert_fusion.4
  152.7 4.4 reshape.429
  157.1 4.8 copy.66
  161.9 11.0 fusion.63
  173.0 7.6 fusion.45
  184.7 4.0 fusion.64
  190.6 69.1 %all-gather.17.cloned.1.call-done = bf16[1024,4096]{1,0:T(8,128)(2,1)} async-done(((bf16[64,4096]{1,0:T(8,128)(2,1)}), bf16[1024,4096]{1,0:T(8,128)(2,1)}) %all-gather.17.cloned.1.call-update) | async-done | bytes 8388624 | tf_op jit(solution)/shard_map/all_gather | solution.py:34
  259.7 11.4 fusion.60
  271.1 63.5 %all-gather.19.cloned.1.call-done = bf16[1024,4096]{1,0:T(8,128)(2,1)} async-done(((bf16[64,4096]{1,0:T(8,128)(2,1)}), bf16[1024,4096]{1,0:T(8,128)(2,1)}) %all-gather.19.cloned.1.call-update) | async-done | bytes 8388624 | tf_op jit(solution)/shard_map/all_gather | solution.py:34
  334.6 34.8 %convert_reduce_fusion = (f32[4096]{0:T(1024)}, bf16[640,4096]{1,0:T(8,128)(2,1)S(1)}, f32[640,4096]{1,0:T(8,128)}) fusion(f32[640,4096]{1,0:T(8,128)} %fusion.60, f32[4096]{0:T(1024)S(1)} %fusion.54, bf16[640,1024]{1,0:T(8,128)(2,1)} %bitcast.173, bf16[1024,4096]{1,0:T(8,128)(2,1)} %all-gather.19.cloned.1.call-done), kind=kOutput, calls=%fused_computation.8 | convolution fusion | flops 5565313024 | bytes 35946496 | tf_op jit(solution)/shard_map/dot_general | solution.py:45
  369.5 6.1 multiply_reduce_fusion.1
  380.9 4.5 reshape.431
  385.4 5.2 copy.72
  390.6 8.6 convert_reduce_fusion.1
  402.0 4.5 reshape.390
  411.8 14.3 %multiply_reduce_fusion = (f32[2,16,320]{2,1,0:T(8,128)S(1)}, f32[2,16,320,320]{2,3,1,0:T(8,128)}) fusion(f32[2,16,320,320]{2,3,1,0:T(8,128)} %get-tuple-element.62, f32[2,16,320]{2,1,0:T(8,128)S(1)} %get-tuple-element.61, bf16[2,320,16,64]{1,3,2,0:T(8,128)(2,1)} %copy.72, bf16[2,320,16,64]{1,3,2,0:T(8,128)(2,1)} %copy.68), kind=kOutput, calls=%fused_computation.2 | convolution fusion | flops 429250560 | bytes 28917760 | tf_op jit(solution)/shard_map/bqhc,bkhc->bhqk/dot_general | solution.py:146
  426.1 11.2 multiply_convert_fusion
  443.2 4.5 reshape.389
  453.0 5.4 convert_reduce_fusion.2
  461.2 4.7 reshape.388
  471.2 3.9 convolution_convert_fusion.1
  477.1 9.7 convolution_convert_fusion
  489.2 6.2 pad_maximum_fusion
  495.5 8.4 multiply_convert_fusion.1
  503.9 7.3 convert_bitcast_fusion
  513.6 6.2 pad_maximum_fusion.1
  527.2 3.9 multiply_reduce_fusion.2
  531.4 39.7 %all-reduce = f32[32,384]{1,0:T(8,128)S(1)} all-reduce(f32[32,384]{1,0:T(8,128)S(1)} %concatenate.7), channel_id=9, replica_groups=mesh['dp'=16,'tensor'=2] {'dp','tensor'}, use_global_device_ids=true, to_apply=%region_20.21.clone | all-reduce | flops 12288 | bytes 98304
  572.3 4.3 add_multiply_fusion
  576.5 10.5 add_convert_fusion.2
  587.0 98.7 %reduce-scatter.9.cloned.1.call-done = bf16[64,512]{1,0:T(8,128)(2,1)} async-done(((bf16[2048,512]{1,0:T(8,128)(2,1)}), bf16[64,512]{1,0:T(8,128)(2,1)}) %reduce-scatter.9.cloned.1.call-update) | async-done | bytes 65552 | tf_op jit(solution)/shard_map/reduce_scatter | solution.py:41
  685.8 137.3 %reduce-scatter.7.cloned.1.call-done = bf16[64,512]{1,0:T(8,128)(2,1)} async-done(((bf16[2048,512]{1,0:T(8,128)(2,1)}), bf16[64,512]{1,0:T(8,128)(2,1)}) %reduce-scatter.7.cloned.1.call-update) | async-done | bytes 65552 | tf_op jit(solution)/shard_map/reduce_scatter | solution.py:41
  824.8 135.1 %reduce-scatter.13.cloned.1.call-done = bf16[64,512]{1,0:T(8,128)(2,1)} async-done(((bf16[2048,512]{1,0:T(8,128)(2,1)}), bf16[64,512]{1,0:T(8,128)(2,1)}) %reduce-scatter.13.cloned.1.call-update) | async-done | bytes 65552 | tf_op jit(solution)/shard_map/reduce_scatter | solution.py:41
  961.4 146.5 %reduce-scatter.15.cloned.1.call-done = bf16[64,2048]{1,0:T(8,128)(2,1)} async-done(((bf16[2048,2048]{1,0:T(8,128)(2,1)}), bf16[64,2048]{1,0:T(8,128)(2,1)}) %reduce-scatter.15.cloned.1.call-update) | async-done | bytes 262160 | tf_op jit(solution)/shard_map/reduce_scatter | solution.py:41
  1109.7 146.7 %reduce-scatter.17.cloned.1.call-done = bf16[64,2048]{1,0:T(8,128)(2,1)} async-done(((bf16[2048,2048]{1,0:T(8,128)(2,1)}), bf16[64,2048]{1,0:T(8,128)(2,1)}) %reduce-scatter.17.cloned.1.call-update) | async-done | bytes 262160 | tf_op jit(solution)/shard_map/reduce_scatter | solution.py:41
  (185 shorter events, 67.5 us)
Async XLA Ops:
  7.2 34.3 %copy-start.15 = (bf16[2048,64]{0,1:T(8,128)(2,1)S(1)}, bf16[2048,64]{0,1:T(8,128)(2,1)}, u32[]{:S(2)}) copy-start(bf16[2048,64]{0,1:T(8,128)(2,1)} %param.30) | copy-start | bytes 786436
  7.2 41.8 %copy-start.35 = (bf16[32]{0:T(256)(128)(2,1)S(1)}, bf16[32]{0:T(256)(128)(2,1)}, u32[]{:S(2)}) copy-start(bf16[32]{0:T(256)(128)(2,1)} %param.31) | copy-start | bytes 196
  7.2 41.8 %copy-start.36 = (bf16[128]{0:T(256)(128)(2,1)S(1)}, bf16[128]{0:T(256)(128)(2,1)}, u32[]{:S(2)}) copy-start(bf16[128]{0:T(256)(128)(2,1)} %param.29) | copy-start | bytes 772
  7.2 41.8 %copy-start.34 = (bf16[32]{0:T(256)(128)(2,1)S(1)}, bf16[32]{0:T(256)(128)(2,1)}, u32[]{:S(2)}) copy-start(bf16[32]{0:T(256)(128)(2,1)} %param.27) | copy-start | bytes 196
  7.2 41.8 %copy-start.33 = (bf16[32]{0:T(256)(128)(2,1)S(1)}, bf16[32]{0:T(256)(128)(2,1)}, u32[]{:S(2)}) copy-start(bf16[32]{0:T(256)(128)(2,1)} %param.26) | copy-start | bytes 196
  7.2 41.8 %copy-start.32 = (bf16[32]{0:T(256)(128)(2,1)S(1)}, bf16[32]{0:T(256)(128)(2,1)}, u32[]{:S(2)}) copy-start(bf16[32]{0:T(256)(128)(2,1)} %param.25) | copy-start | bytes 196
  7.2 41.8 %copy-start.31 = (bf16[32]{0:T(256)(128)(2,1)S(1)}, bf16[32]{0:T(256)(128)(2,1)}, u32[]{:S(2)}) copy-start(bf16[32]{0:T(256)(128)(2,1)} %param.23) | copy-start | bytes 196
  7.3 41.8 %copy-start.30 = (bf16[32]{0:T(256)(128)(2,1)S(1)}, bf16[32]{0:T(256)(128)(2,1)}, u32[]{:S(2)}) copy-start(bf16[32]{0:T(256)(128)(2,1)} %param.22) | copy-start | bytes 196
  7.3 41.8 %copy-start.29 = (bf16[32]{0:T(256)(128)(2,1)S(1)}, bf16[32]{0:T(256)(128)(2,1)}, u32[]{:S(2)}) copy-start(bf16[32]{0:T(256)(128)(2,1)} %param.20) | copy-start | bytes 196
  7.3 41.8 %copy-start.28 = (bf16[32]{0:T(256)(128)(2,1)S(1)}, bf16[32]{0:T(256)(128)(2,1)}, u32[]{:S(2)}) copy-start(bf16[32]{0:T(256)(128)(2,1)} %param.19) | copy-start | bytes 196
  7.3 41.9 %copy-start.41 = (s32[4]{0:T(128)S(1)}, s32[4]{0:T(128)}, u32[]{:S(2)}) copy-start(s32[4]{0:T(128)} %param.17) | copy-start | bytes 52
  7.3 42.1 %copy-start.1 = (bf16[2,320,1024]{2,1,0:T(8,128)(2,1)S(1)}, bf16[2,320,1024]{2,1,0:T(8,128)(2,1)}, u32[]{:S(2)}) copy-start(bf16[2,320,1024]{2,1,0:T(8,128)(2,1)} %param.16) | copy-start | bytes 3932164
  7.3 112.7 %all-gather.25.cloned.1.call-start = ((), (), s32[]{:S(2)}) async-start(), calls=%async_computation.17 | async-start | bytes 2228224 | tf_op jit(solution)/shard_map/all_gather | solution.py:34
  14.4 119.2 %all-gather.21.cloned.1.call-start = ((), (), s32[]{:S(2)}) async-start(), calls=%async_computation.15 | async-start | bytes 2228224 | tf_op jit(solution)/shard_map/all_gather | solution.py:34
  19.5 128.5 %all-gather.23.cloned.1.call-start = ((), (), s32[]{:S(2)}) async-start(), calls=%async_computation.16 | async-start | bytes 2228224 | tf_op jit(solution)/shard_map/all_gather | solution.py:34
  24.7 160.0 %all-gather.15.cloned.1.call-start = ((), (), s32[]{:S(2)}) async-start(), calls=%async_computation.6 | async-start | bytes 2228224 | tf_op jit(solution)/shard_map/all_gather | solution.py:34
  32.1 227.6 %all-gather.17.cloned.1.call-start = ((), (), s32[]{:S(2)}) async-start(), calls=%async_computation.7 | async-start | bytes 8912896 | tf_op jit(solution)/shard_map/all_gather | solution.py:34
  41.5 293.2 %all-gather.19.cloned.1.call-start = ((), (), s32[]{:S(2)}) async-start(), calls=%async_computation.8 | async-start | bytes 8912896 | tf_op jit(solution)/shard_map/all_gather | solution.py:34
  48.9 538.1 %reduce-scatter.11.cloned.1.call-start = ((), (), s32[]{:S(2)}) async-start(), calls=%async_computation.11 | async-start | bytes 2162688 | tf_op jit(solution)/shard_map/reduce_scatter | solution.py:41
  49.4 135.3 %copy-start.19 = (f32[640]{0:T(1024)}, f32[640]{0:T(1024)S(1)}, u32[]{:S(2)}) copy-start(f32[640]{0:T(1024)S(1)} %reshape.408) | copy-start | bytes 7684
  49.9 70.0 %copy-start.21 = (f32[640]{0:T(1024)}, f32[640]{0:T(1024)S(1)}, u32[]{:S(2)}) copy-start(f32[640]{0:T(1024)S(1)} %div.35) | copy-start | bytes 7684
  50.6 69.4 %copy-start.23 = (f32[640]{0:T(1024)}, f32[640]{0:T(1024)S(1)}, u32[]{:S(2)}) copy-start(f32[640]{0:T(1024)S(1)} %rsqrt.21) | copy-start | bytes 7684
  117.2 2.7 copy-start.16
  117.3 142.4 %copy-start.26 = (f32[1024]{0:T(1024)}, f32[1024]{0:T(1024)S(1)}, u32[]{:S(2)}) copy-start(f32[1024]{0:T(1024)S(1)} %reshape.415) | copy-start | bytes 12292
  120.0 4.6 copy-start.12
  133.6 28.4 %copy-start.7 = (bf16[2,320,16,64]{1,3,2,0:T(8,128)(2,1)}, bf16[2,320,16,64]{1,3,2,0:T(8,128)(2,1)S(1)}, u32[]{:S(2)}) copy-start(bf16[2,320,16,64]{1,3,2,0:T(8,128)(2,1)S(1)} %copy.67) | copy-start | bytes 3932164
  334.6 34.8 %copy-start.4 = (f32[640,1024]{1,0:T(8,128)S(1)}, f32[640,1024]{1,0:T(8,128)}, u32[]{:S(2)}) copy-start(f32[640,1024]{1,0:T(8,128)} %copy-done.3) | copy-start | bytes 7864324
  334.6 34.8 %copy-start.37 = (bf16[1024,4096]{1,0:T(8,128)(2,1)S(1)}, bf16[1024,4096]{1,0:T(8,128)(2,1)}, u32[]{:S(2)}) copy-start(bf16[1024,4096]{1,0:T(8,128)(2,1)} %all-gather.17.cloned.1.call-done) | copy-start | bytes 25165828
  369.5 6.1 copy-start.42
  369.5 6.1 copy-start.10
  375.6 2.7 copy-start.40
  411.8 274.0 %reduce-scatter.9.cloned.1.call-start = ((), (), s32[]{:S(2)}) async-start(), calls=%async_computation.10 | async-start | bytes 2162688 | tf_op jit(solution)/shard_map/reduce_scatter | solution.py:41
  426.1 11.2 copy-start.8
  437.3 3.0 copy-start
  452.9 370.2 %reduce-scatter.7.cloned.1.call-start = ((), (), s32[]{:S(2)}) async-start(), calls=%async_computation.9 | async-start | bytes 2162688 | tf_op jit(solution)/shard_map/reduce_scatter | solution.py:41
  471.2 488.7 %reduce-scatter.13.cloned.1.call-start = ((), (), s32[]{:S(2)}) async-start(), calls=%async_computation.12 | async-start | bytes 2162688 | tf_op jit(solution)/shard_map/reduce_scatter | solution.py:41
  475.4 1.7 copy-start.27
  477.0 630.9 %reduce-scatter.15.cloned.1.call-start = ((), (), s32[]{:S(2)}) async-start(), calls=%async_computation.13 | async-start | bytes 8650752 | tf_op jit(solution)/shard_map/reduce_scatter | solution.py:41
  495.5 760.9 %reduce-scatter.17.cloned.1.call-start = ((), (), s32[]{:S(2)}) async-start(), calls=%async_computation.14 | async-start | bytes 8650752 | tf_op jit(solution)/shard_map/reduce_scatter | solution.py:41
  495.5 8.4 copy-start.11
  503.9 7.3 copy-start.9
  521.0 3.7 copy-start.14
  521.0 3.7 copy-start.39
  524.7 1.7 copy-start.13
  524.7 1.7 copy-start.17
  524.8 2.4 copy-start.38
  527.2 4.1 copy-start.25
  572.2 4.3 copy-start.5
  (7 other events, 10.5 us)
Sparse Core Ops, SparseCore 0:
  14.5 43.2 all-gather.24
  60.0 40.1 all-gather.20
  102.4 40.0 all-gather.22
  144.5 40.1 all-gather.14
  186.7 72.9 all-gather.16
  261.7 72.8 all-gather.18
  411.9 137.2 reduce-scatter.10
  551.5 134.2 reduce-scatter.8
  688.0 135.0 reduce-scatter.6
  825.2 134.6 reduce-scatter.12
  962.2 145.6 reduce-scatter.14
  1110.0 146.2 reduce-scatter.16

commit v2 on v1

--- a/solution.py
+++ b/solution.py
@@ -1,13 +1,378 @@
+import functools
+import math
+
 import jax
 import jax.numpy as jnp
 from jax import lax
+from jax.experimental import pallas as pl
+from jax.experimental.pallas import tpu as pltpu
 from jax.sharding import PartitionSpec as P
 
 HEAD_DIM = 64
 EPSILON = 1e-06
 BOTH = ("dp", "tensor")
+MESH = pl.DeviceIdType.MESH
+LANES = 128
 bf16 = jnp.bfloat16
 f32 = jnp.float32
+
+
+class Place:
+    def __init__(self, dp_count):
+        self.bits = int(math.log2(dp_count))
+        self.dp = lax.axis_index("dp")
+        self.tensor = lax.axis_index("tensor")
+        self.own = [lax.rem(lax.div(self.dp, 2**k), 2) for k in range(self.bits)]
+
+    def partner(self, stage):
+        if stage == "t":
+            return {"tensor": 1 - self.tensor}
+        return {"dp": self.dp + (1 - 2 * self.own[stage]) * 2**stage}
+
+    def greet(self):
+        barrier = pltpu.get_barrier_semaphore()
+        stages = list(range(self.bits)) + ["t"]
+        for stage in stages:
+            pl.semaphore_signal(barrier, inc=1, device_id=self.partner(stage), device_id_type=MESH)
+        pl.semaphore_wait(barrier, len(stages))
+
+    def lead(self, done, flipped=None):
+        index = []
+        for bit in range(self.bits - 1, -1, -1):
+            if bit in done:
+                index.append(slice(None))
+            elif bit == flipped:
+                index.append(1 - self.own[bit])
+            else:
+                index.append(self.own[bit])
+        return tuple(index)
+
+
+def stage_orders(bits):
+    far = list(range(bits - 1, 1, -1))
+    return (far + [1, "t"], far + ["t", 1], [1] + far + ["t"], ["t"] + far + [1])
+
+
+class Spread:
+    def __init__(self, place, shard, full, half, first, count, order, sems, base):
+        self.place, self.shard, self.full = place, shard, full
+        self.half, self.first, self.count, self.order = half, first, count, order
+        self.send, self.recv, self.local = sems
+        self.slot = base
+        self.stages = len(order)
+        self.plane = [None] * self.stages
+        self.across = []
+
+    @staticmethod
+    def slots(order):
+        total, twice = 1, 1
+        for stage in order:
+            total += twice
+            total += twice
+            if stage == "t":
+                twice = 2
+        return total
+
+    def columns(self, which):
+        return pl.ds(pl.multiple_of(which * self.half + self.first, 128), self.count)
+
+    def views(self, done, flipped=None):
+        place = self.place
+        if "t" in done:
+            sides = [0, 1]
+        elif flipped == "t":
+            sides = [1 - place.tensor]
+        else:
+            sides = [place.tensor]
+        lead = place.lead(done, flipped)
+        return [self.full.at[lead + (slice(None), self.columns(side))] for side in sides]
+
+    def post(self, src, dst, stage):
+        made = pltpu.make_async_remote_copy(
+            src_ref=src,
+            dst_ref=dst,
+            send_sem=self.send.at[self.slot],
+            recv_sem=self.recv.at[self.slot],
+            device_id=self.place.partner(stage),
+            device_id_type=MESH,
+        )
+        self.slot += 1
+        made.start()
+        return made
+
+    def piece(self):
+        return self.shard.at[:, pl.ds(self.first, self.count)]
+
+    def tick(self, step):
+        order = self.order
+        if step == 0:
+            (target,) = self.views(set())
+            self.keep = pltpu.make_async_copy(self.piece(), target, self.local)
+            self.keep.start()
+            self.plane[0] = [self.post(self.piece(), target, order[0])]
+            self.across.append(self.post(self.piece(), target, 0))
+            return
+        for made in self.plane[step - 1]:
+            made.wait_recv()
+        if step == 1:
+            self.keep.wait()
+        before = set(order[: step - 1])
+        if step < self.stages:
+            held = self.views(before | {order[step - 1]})
+            self.plane[step] = [self.post(view, view, order[step]) for view in held]
+        fresh = self.views(before, order[step - 1])
+        self.across.extend(self.post(view, view, 0) for view in fresh)
+
+    def finish(self):
+        for group in self.plane:
+            for made in group:
+                made.wait_send()
+        for made in self.across:
+            made.wait()
+
+
+def spread_kernel(plan, dp_count, names, *refs):
+    count = names
+    shards, fulls = refs[:count], refs[count : 2 * count]
+    send, recv, local = refs[2 * count :]
+    place = Place(dp_count)
+    place.greet()
+    orders = stage_orders(place.bits)
+    flows, base = [], 0
+    for index, (matrix, first, columns, which, begin) in enumerate(plan):
+        order = orders[which]
+        shard = shards[matrix]
+        sems = (send, recv, local.at[index])
+        flows.append(
+            (begin, Spread(place, shard, fulls[matrix], shard.shape[1], first, columns, order, sems, base))
+        )
+        base += Spread.slots(order)
+    last = max(begin for begin, _ in flows) + len(orders[0])
+    for tick in range(last + 1):
+        for begin, flow in flows:
+            if 0 <= tick - begin <= flow.stages:
+                flow.tick(tick - begin)
+    for _, flow in flows:
+        flow.finish()
+
+
+def spread_matrices(shards, plan, collective_id):
+    dp_count = lax.axis_size("dp")
+    bits = int(math.log2(dp_count))
+    orders = stage_orders(bits)
+    slots = sum(Spread.slots(orders[entry[3]]) for entry in plan)
+    sent = 0
+    fulls = pl.pallas_call(
+        functools.partial(spread_kernel, plan, dp_count, len(shards)),
+        out_shape=[
+            jax.ShapeDtypeStruct((2,) * bits + (s.shape[0], 2 * s.shape[1]), s.dtype) for s in shards
+        ],
+        in_specs=[pl.BlockSpec(memory_space=pltpu.VMEM)] * len(shards),
+        out_specs=[pl.BlockSpec(memory_space=pl.ANY)] * len(shards),
+        scratch_shapes=[
+            pltpu.SemaphoreType.DMA((slots,)),
+            pltpu.SemaphoreType.DMA((slots,)),
+            pltpu.SemaphoreType.DMA((len(plan),)),
+        ],
+        compiler_params=pltpu.CompilerParams(collective_id=collective_id, has_side_effects=True, vmem_limit_bytes=8 << 20),
+        name="spread_weights",
+    )(*shards)
+    return [f.reshape(dp_count * s.shape[0], 2 * s.shape[1]) for f, s in zip(fulls, shards)]
+
+
+class Fold:
+    def __init__(self, place, partial, half, first, count, order, refs, sems, base):
+        self.place, self.partial = place, partial
+        self.half, self.first, self.count = half, first, count
+        self.order = list(reversed(order))
+        self.total, self.landing, self.result = refs
+        self.send, self.recv, self.local = sems
+        self.slot = base
+        self.stages = len(order)
+        self.copies = []
+
+    @staticmethod
+    def slots(order):
+        return 2 + len(order)
+
+    def post(self, src, dst, stage):
+        made = pltpu.make_async_remote_copy(
+            src_ref=src,
+            dst_ref=dst,
+            send_sem=self.send.at[self.slot],
+            recv_sem=self.recv.at[self.slot],
+            device_id=self.place.partner(stage),
+            device_id_type=MESH,
+        )
+        self.slot += 1
+        made.start()
+        return made
+
+    def begin(self):
+        place = self.place
+        every = set(range(1, place.bits))
+        self.loads, self.cores = [], []
+        for side in (0, 1):
+            columns = pl.ds(side * self.half + self.first, self.count)
+            mine = self.partial.at[place.lead(every) + (slice(None), columns)]
+            theirs = self.partial.at[place.lead(every, 0) + (slice(None), columns)]
+            self.cores.append(self.post(theirs, self.landing[0].at[side], 0))
+            load = pltpu.make_async_copy(mine, self.total.at[side], self.local.at[side])
+            load.start()
+            self.loads.append(load)
+
+    def where(self, done, last=None):
+        place = self.place
+        index = []
+        for name in ["t"] + list(range(place.bits - 1, 0, -1)):
+            own = place.tensor if name == "t" else place.own[name]
+            if name in done:
+                index.append(own)
+            elif name == last:
+                index.append(1 - own)
+            else:
+                index.append(None)
+        return index
+
+    def add(self, landing, done):
+        index = self.where(done)
+        free = [i for i, entry in enumerate(index) if entry is None]
+        size = 2 ** len(free)
+
+        def one(j, carry):
+            spots, inner = list(index), []
+            for position, dim in enumerate(free):
+                bit = lax.rem(lax.div(j, 2 ** (len(free) - 1 - position)), 2)
+                spots[dim] = bit
+                inner.append(bit)
+            spots, inner = tuple(spots), tuple(inner)
+            value = self.total[spots].astype(f32) + landing[inner].astype(f32)
+            self.total[spots] = value.astype(self.total.dtype)
+            return carry
+
+        lax.fori_loop(0, size, one, 0)
+
+    def tick(self, step):
+        order = self.order
+        if step == 0:
+            for load in self.loads:
+                load.wait()
+            for made in self.cores:
+                made.wait_recv()
+            self.add(self.landing[0], set())
+        else:
+            self.copies[step - 1].wait_recv()
+            if step < self.stages:
+                self.add(self.landing[step], set(order[:step]))
+            else:
+                spots = tuple(self.where(set(order)))
+                value = self.total[spots].astype(f32) + self.landing[step][...].astype(f32)
+                self.result[:, self.first : self.first + self.count] = value
+        if step < self.stages:
+            index = self.where(set(order[:step]), order[step])
+            view = self.total.at[tuple(slice(None) if e is None else e for e in index)]
+            self.copies.append(self.post(view, self.landing[step + 1], order[step]))
+
+    def finish(self):
+        for made in self.cores + self.copies:
+            made.wait_send()
+
+
+def fold_scratch(bits, rows, count, dtype):
+    lead = (2,) * bits
+    shapes = [pltpu.VMEM(lead + (rows, count), dtype)]
+    shapes.append(pltpu.VMEM(lead + (rows, count), dtype))
+    for stage in range(1, bits + 1):
+        shapes.append(pltpu.VMEM(lead[stage:] + (rows, count), dtype))
+    return shapes
+
+
+def fold_kernel(plan, dp_count, count, *refs):
+    place = Place(dp_count)
+    bits = place.bits
+    partials, results = refs[:count], refs[count : 2 * count]
+    send, recv, local = refs[2 * count : 2 * count + 3]
+    buffers = refs[2 * count + 3 :]
+    place.greet()
+    orders = stage_orders(bits)
+    flows, base = [], 0
+    for index, (matrix, first, columns, which, begin) in enumerate(plan):
+        order = orders[which]
+        mine = buffers[index * (bits + 2) : (index + 1) * (bits + 2)]
+        half = partials[matrix].shape[-1] // 2
+        sems = (send, recv, local.at[index])
+        refs_here = (mine[0], mine[1:], results[matrix])
+        flow = Fold(place, partials[matrix], half, first, columns, order, refs_here, sems, base)
+        flows.append((begin, flow))
+        base += Fold.slots(order)
+    for _, flow in flows:
+        flow.begin()
+    last = max(begin for begin, _ in flows) + len(orders[0])
+    for tick in range(last + 1):
+        for begin, flow in flows:
+            if 0 <= tick - begin <= flow.stages:
+                flow.tick(tick - begin)
+    for _, flow in flows:
+        flow.finish()
+
+
+def fold_matrices(partials, plan, collective_id):
+    dp_count = lax.axis_size("dp")
+    bits = int(math.log2(dp_count))
+    orders = stage_orders(bits)
+    slots = sum(Fold.slots(orders[entry[3]]) for entry in plan)
+    views = []
+    for p in partials:
+        rows = p.shape[0] // dp_count
+        views.append(p.reshape((2,) * bits + (rows, p.shape[1])))
+    scratch = [
+        pltpu.SemaphoreType.DMA((slots,)),
+        pltpu.SemaphoreType.DMA((slots,)),
+        pltpu.SemaphoreType.DMA((len(plan), 2)),
+    ]
+    for matrix, first, columns, which, begin in plan:
+        scratch += fold_scratch(bits, views[matrix].shape[-2], columns, views[matrix].dtype)
+    return pl.pallas_call(
+        functools.partial(fold_kernel, plan, dp_count, len(views)),
+        out_shape=[jax.ShapeDtypeStruct((v.shape[-2], v.shape[-1] // 2), f32) for v in views],
+        in_specs=[pl.BlockSpec(memory_space=pl.ANY)] * len(views),
+        out_specs=[pl.BlockSpec(memory_space=pltpu.VMEM)] * len(views),
+        scratch_shapes=scratch,
+        compiler_params=pltpu.CompilerParams(
+            collective_id=collective_id, has_side_effects=True, vmem_limit_bytes=56 << 20
+        ),
+        name="fold_grads",
+    )(*views)
+
+
+def make_plan(sizes, fractions):
+    plan, position, tick = [], {}, 0
+    for matrix, size in sizes:
+        start = position.get(matrix, 0)
+        units, total, taken, gone = size // 128, sum(fractions), 0, 0
+        for which, weight in enumerate(fractions):
+            taken += weight
+            upto = (units * taken * 2 + total) // (2 * total)
+            if upto > gone:
+                plan.append((matrix, start + gone * 128, (upto - gone) * 128, which, tick))
+            gone = upto
+        position[matrix] = start + size
+        tick += 1
+    return plan
+
+
+EVEN = (1, 1, 1, 1)
+
+
+def chunks(order, halves):
+    sizes = []
+    for matrix in order:
+        half = halves[matrix]
+        if half > 1536:
+            sizes += [(matrix, half // 2)] * 2
+        else:
+            sizes.append((matrix, half))
+    return sizes
 
 
 def exact_gelu(values):
@@ -27,18 +392,6 @@
     mean_z = jnp.mean(z, axis=-1, keepdims=True)
     mean_zx = jnp.mean(z * unit, axis=-1, keepdims=True)
     return scale * (z - mean_z - unit * mean_zx)
-
-
-def gather_matrix(shard):
-    wide = lax.all_gather(shard, "tensor", axis=1, tiled=True)
-    return lax.all_gather(wide, "dp", axis=0, tiled=True)
-
-
-def scatter_matrix(grad):
-    rows, columns = grad.shape
-    halves = jnp.stack(jnp.split(grad, lax.axis_size("tensor"), axis=1))
-    halves = halves.reshape(-1, columns // lax.axis_size("tensor"))
-    return lax.psum_scatter(halves, ("tensor", "dp"), scatter_dimension=0, tiled=True)
 
 
 def mm(a, b, dims):
@@ -87,20 +440,28 @@
         up_bias,
     )
     sizes = [v.shape[0] for v in vectors]
-    packed = lax.all_gather(jnp.concatenate(vectors), BOTH, axis=0)
+    packed = jnp.concatenate(vectors)
+    length = -(-packed.shape[0] // LANES) * LANES
+    packed = jnp.pad(packed, (0, length - packed.shape[0]))
+    part = width // lax.axis_size("tensor")
+    row_count = qkv_weight.shape[1]
+    shards_here = [
+        qkv_weight.transpose(1, 0, 2).reshape(row_count, 3 * part),
+        out_weight.T,
+        up_weight,
+        down_weight.T,
+        jnp.broadcast_to(packed, (8, length)),
+    ]
+    halves = [s.shape[1] for s in shards_here]
+    plan = [(4, 0, length, 2, 0)] + make_plan(chunks((0, 1, 2, 3), halves), EVEN)
+    qkv_w, out_t, up_w, down_t, spread = spread_matrices(shards_here, plan, 1)
+    spread = spread.reshape(-1, 8, 2, length)[:, 0].reshape(device_count, length)
     full = []
     start = 0
     for size in sizes:
-        full.append(packed[:, start : start + size].reshape(-1).astype(f32))
+        full.append(spread[:, start : start + size].reshape(-1).astype(f32))
         start += size
     gain_one, shift_one, qbias, vbias, obias, gain_two, shift_two, dbias, ubias = full
-
-    query_w = gather_matrix(qkv_weight[0])
-    key_w = gather_matrix(qkv_weight[1])
-    value_w = gather_matrix(qkv_weight[2])
-    out_t = gather_matrix(out_weight.T)
-    up_w = gather_matrix(up_weight)
-    down_t = gather_matrix(down_weight.T)
 
     positions = jnp.arange(slot_count, dtype=jnp.int32)
     own_lengths = lax.dynamic_slice_in_dim(lengths, tensor_rank * image_count, image_count)
@@ -113,9 +474,10 @@
     def split(rows):
         return rows.reshape(image_count, slot_count, heads, HEAD_DIM)
 
-    query = split((mm(first, query_w, NN) + qbias).astype(bf16))
-    key = split(mm(first, key_w, NN).astype(bf16))
-    value = split((mm(first, value_w, NN) + vbias).astype(bf16))
+    rows = mm(first, qkv_w, NN).reshape(tokens, 2, 3, part)
+    query = split((rows[:, :, 0].reshape(tokens, width) + qbias).astype(bf16))
+    key = split(rows[:, :, 1].reshape(tokens, width).astype(bf16))
+    value = split((rows[:, :, 2].reshape(tokens, width) + vbias).astype(bf16))
     scores = jnp.einsum("bqhc,bkhc->bhqk", query, key, preferred_element_type=f32) * score_scale
     scores = jnp.where(valid[:, None, None, :], scores, -1000000000.0)
     highest = jnp.max(scores, axis=-1, keepdims=True)
@@ -133,15 +495,15 @@
 
     grad_low = cotangent.reshape(tokens, width)
     grad_out = grad_low.astype(f32)
-    down_grad = scatter_matrix(mm(grad_low, active, TN).astype(bf16))
+    down_part = mm(grad_low, active, TN).astype(bf16)
     grad_active = mm(grad_low, down_t, NN)
     grad_hidden32 = jax.vjp(exact_gelu, hidden)[1](grad_active)[0]
     grad_hidden = grad_hidden32.astype(bf16)
-    up_grad = scatter_matrix(mm(second, grad_hidden, TN).astype(bf16))
+    up_part = mm(second, grad_hidden, TN).astype(bf16)
     grad_second = mm(grad_hidden, up_w, NT)
     grad_middle = grad_out + norm_back(grad_second, unit_two, scale_two, gain_two)
     grad_attn = grad_middle.astype(bf16)
-    out_grad = scatter_matrix(mm(grad_attn, mixed, TN).astype(bf16))
+    out_part = mm(grad_attn, mixed, TN).astype(bf16)
     grad_mixed = split(mm(grad_attn, out_t, NN).astype(bf16))
     grad_weights = jnp.einsum("bqhc,bkhc->bhqk", grad_mixed, value, preferred_element_type=f32)
     value_grad = jnp.einsum("bhqk,bqhc->bkhc", weights_low, grad_mixed, preferred_element_type=f32)
@@ -156,14 +518,11 @@
     )
     query_grad = query_grad.astype(bf16).reshape(tokens, width)
     key_grad = key_grad.astype(bf16).reshape(tokens, width)
-    qkv_grad = jnp.stack(
-        [
-            scatter_matrix(mm(first, query_grad, TN).astype(bf16)),
-            scatter_matrix(mm(first, key_grad, TN).astype(bf16)),
-            scatter_matrix(mm(first, value_grad, TN).astype(bf16)),
-        ]
-    )
-    grad_first = mm(query_grad, query_w, NT) + mm(key_grad, key_w, NT) + mm(value_grad, value_w, NT)
+    grad_rows = jnp.stack(
+        [g.reshape(tokens, 2, part) for g in (query_grad, key_grad, value_grad)], axis=2
+    ).reshape(tokens, 3 * width)
+    qkv_part = mm(first, grad_rows, TN).astype(bf16)
+    grad_first = mm(grad_rows, qkv_w, NT)
     grad_in = norm_back(grad_first, unit_one, scale_one, gain_one)
     input_grad = (grad_middle + grad_in) * valid_rows
 
@@ -182,7 +541,15 @@
         total(grad_hidden),
     )
     stacked = jnp.concatenate([v.reshape(device_count, -1) for v in vector_grads], axis=1)
-    own = lax.psum_scatter(stacked, BOTH, scatter_dimension=0, tiled=True)[0]
+    stacked = jnp.pad(stacked, ((0, 0), (0, length - stacked.shape[1])))
+    stacked = stacked.reshape(-1, 1, 2 * length)
+    stacked = jnp.pad(stacked, ((0, 0), (0, 7), (0, 0))).reshape(-1, 2 * length)
+    plan = make_plan(chunks((3, 2, 1, 0), halves), EVEN)
+    plan = plan + [(4, 0, length, 2, 0)]
+    qkv_grad, out_grad, up_grad, down_grad, own = fold_matrices(
+        [qkv_part, out_part, up_part, down_part, stacked], plan, 2
+    )
+    own = own[0]
     shares = []
     start = 0
     for size in sizes:
@@ -194,16 +561,16 @@
         input_grad.reshape(inputs.shape),
         shares[0],
         shares[1],
-        qkv_grad.astype(f32),
+        qkv_grad.reshape(row_count, 3, part).transpose(1, 0, 2),
         shares[2],
         shares[3],
-        out_grad.T.astype(f32),
+        out_grad.T,
         shares[4],
         shares[5],
         shares[6],
-        up_grad.astype(f32),
+        up_grad,
         shares[8],
-        down_grad.T.astype(f32),
+        down_grad.T,
         shares[7],
     )
 

time: 1270 us -> 560 us (0.44)
  waiting for transfers between devices: 798 us -> 0 us
  Pallas kernels: 0 us -> 242 us
  blocking collectives: 146 us -> 0 us
  other arithmetic: 55.1 us -> 25.2 us
  local copies, waits for them, and re-layouts: 77 us -> 103 us
  between operations: 15.1 us -> 1.54 us
    reduce_scatter x6 -> x0, waiting for transfers between devices: 664 us -> none  [scatter_matrix(): lax.psum_scatter(halves, ('tensor', 'dp'), scatter_dimension=0, tiled=True)]
    pallas_call x0 -> x2, Pallas kernels: none -> 242 us  [the longest x1 126 us: fold_matrices(): pl.pallas_call(functools.partial(fold_kernel, plan, dp_count, len(views))...]
    all_gather x6 -> x0, waiting for transfers between devices: 133 us -> none  [gather_matrix(): return lax.all_gather(wide, 'dp', axis=0, tiled=True)]
    all_gather x7 -> x0, blocking collectives: 106 us -> none  [the longest x1 65.8 us: shards(): packed = lax.all_gather(jnp.concatenate(vectors), BOTH, axis=0)]
    unnamed x1 -> x0, blocking collectives: 39.7 us -> none
    reshape x8 -> x2, local copies, waits for them, and re-layouts: 37 us -> 7.45 us  [split(): return rows.reshape(image_count, slot_count, heads, HEAD_DIM)]
    another operation x6 -> x1, other arithmetic: 18.6 us -> 1.95 us  [shards(): jnp.stack([g.reshape(tokens, 2, part) for g in (query_grad, key_grad, val...]
    another operation x6 -> x7, local copies, waits for them, and re-layouts: 5.46 us -> 21.4 us  [the longest x4 11 us: shards(): jnp.stack([g.reshape(tokens, 2, part) for g in (query_grad, key_grad, val...]
  transfers between devices with their start and end apart: 12 -> 0, of which waited for: 8 -> 0; matrix products, arithmetic and copies ran while one was open for 18% -> 0% of each run, Pallas kernels for 0% -> 0%
where the time goes in v2:
time: 560 us; the launch traced here: 549 us
  Pallas kernels  242 us (43%)
  matrix products  178 us (32%)
  local copies, waits for them, and re-layouts  103 us (18%)
  other arithmetic  25.2 us (4%)
    dot_general x12, matrix products, mm(): return lax.dot_general(a, b, (dims, ((), ())), preferred_element_type=f32)  127 us
    pallas_call x1, Pallas kernels, fold_matrices(): pl.pallas_call(functools.partial(fold_kernel, plan, dp_count, len(views))...  126 us
    pallas_call x1, Pallas kernels, spread_matrices(): pl.pallas_call(functools.partial(spread_kernel, plan, dp_count, len(shard...  116 us
    unnamed x88, local copies, waits for them, and re-layouts  19.6 us
    dot_general x1, matrix products, shards(): jnp.einsum('bqhc,bkhc->bhqk', grad_mixed, value, preferred_element_type=f32)  15.3 us
    sub x1, matrix products, shards(): shifted = jnp.exp(scores - highest)  11.8 us

profile of v2, /device:TPU:0, one launch (start us, length us, event | category | flops | bytes accessed | tf_op | source)
XLA Modules:
  0.0 549.4 jit_solution(16820942235099218862)
XLA Ops:
  1.5 1.7 fusion.25
  3.3 1.9 multiply_reduce_fusion.6
  6.1 6.1 %concatenate.6 = bf16[384]{0:T(512)(128)(2,1)S(1)} concatenate(bf16[32]{0:T(256)(128)(2,1)} %param.19, bf16[32]{0:T(256)(128)(2,1)} %param.20, bf16[32]{0:T(256)(128)(2,1)} %param.22, bf16[32]{0:T(256)(128)(2,1)} %param.23, bf16[32]{0:T(256)(128)(2,1)} %param.25, bf16[32]{0:T(256)(128)(2,1)} %param.26, bf16[32]{0:T(256)(128)(2,1)} %param.27, bf16[32]{0:T(256)(128)(2,1)} %param.31, ...), dimensions={0} | concatenate | bytes 1536 | tf_op jit(solution)/shard_map/concatenate | solution.py:443
  13.1 116.0 %spread_weights.1 = (bf16[2,2,2,2,64,3072]{5,4,3,2,1,0:T(8,128)(2,1)S(1)}, bf16[2,2,2,2,64,1024]{5,4,3,2,1,0:T(8,128)(2,1)S(1)}, bf16[2,2,2,2,64,4096]{5,4,3,2,1...) custom-call(bf16[64,1536]{1,0:T(8,128)(2,1)S(1)} %bitcast.143, ...), custom_call_target="tpu_custom_call" | custom-call | tf_op jit(solution)/shard_map/spread_weights/pallas_call | solution.py:165
  129.1 2.6 copy-done
  131.7 3.3 copy-done.4
  135.0 3.3 copy-done.5
  139.3 1.9 add_convert_fusion.2
  141.3 9.1 %copy.67 = bf16[3072,1024]{1,0:T(8,128)(2,1)} copy(bf16[3072,1024]{0,1:T(8,128)(2,1)} %bitcast.141) | data formatting | bytes 12582912 | tf_op jit(solution)/shard_map/dot_general | solution.py:398
  150.5 6.6 %fusion.72 = f32[640,2,3,512]{3,0,2,1:T(8,128)S(1)} fusion(bf16[640,1024,1,1]{1,0,3,2:T(8,128)(2,1)S(1)} %bitcast.165, bf16[2,3,512,1024]{3,2,1,0:T(8,128)(2,1)} %bitcast.155), kind=kOutput, calls=%fused_computation.127 | convolution fusion | flops 4026531840 | bytes 15466496 | tf_op jit(solution)/shard_map/dot_general | solution.py:398
  157.1 3.4 fusion.61
  161.7 3.3 copy.70
  165.0 5.2 reshape_squeeze.12
  170.2 1.9 slice.170
  173.6 4.7 convert_element_type.239
  178.3 11.8 %fusion.62 = (f32[2,16,320]{2,1,0:T(8,128)S(1)}, f32[2,16,320,320]{2,3,1,0:T(8,128)}) fusion(pred[2,320]{1,0:T(4,128)(4,1)S(1)} %get-tuple-element.95, bf16[2,320,16,64]{1,0,3,2:T(2,128)(2,1)} %convert_element_type.239, f32[2,320,16,64]{1,0,3,2:T(2,128)} %reshape_squeeze.12, f32[16,64]{1,0:T(8,128)S(1)} %reshape.407), kind=kOutput, calls=%fused_computation.125 | convolution fusion | flops 433848640 | bytes 17085056 | tf_op jit(solution)/shard_map/sub | solution.py:484
  190.1 3.2 copy.68
  193.3 5.2 reshape_squeeze.11
  199.2 8.1 %fusion.39 = bf16[2,320,16,64]{1,3,2,0:T(8,128)(2,1)S(1)} fusion(f32[2,320,16,64]{1,0,3,2:T(2,128)} %reshape_squeeze.11, f32[16,64]{1,0:T(8,128)S(1)} %reshape.406, f32[2,16,320,320]{2,3,1,0:T(8,128)} %get-tuple-element.98, f32[2,16,320]{2,1,0:T(8,128)S(1)} %get-tuple-element.97), kind=kOutput, calls=%fused_computation.83 | convolution fusion | flops 427950080 | bytes 17084416 | tf_op jit(solution)/shard_map/bhqk,bkhc->bqhc/dot_general | solution.py:487
  207.3 2.8 copy.75
  210.1 4.6 reshape.378
  214.9 3.3 fusion.67
  220.2 33.8 %multiply_convert_fusion.1 = (bf16[640,4096]{1,0:T(8,128)(2,1)}, f32[640,4096]{1,0:T(8,128)}, f32[640,4096]{1,0:T(8,128)}) fusion(f32[4096]{0:T(1024)S(1)} %fusion.53, bf16[1024,4096]{1,0:T(8,128)(2,1)} %bitcast.149, f32[640,1024]{1,0:T(8,128)} %copy-done.10, f32[1024]{0:T(1024)S(1)} %reshape.410, f32[1024]{0:T(1024)S(1)} %reshape.409, ...), kind=kOutput, calls=%fused_computation.18 | convolution fusion | flops 5545000960 | bytes 37254144 | tf_op jit(solution)/shard_map/dot_general | solution.py:398
  254.1 17.4 %convert_reduce_fusion = (f32[4096]{0:T(1024)S(1)}, bf16[640,4096]{1,0:T(8,128)(2,1)}) fusion(f32[640,4096]{1,0:T(8,128)} %get-tuple-element.76, bf16[640,1024]{1,0:T(8,128)(2,1)S(1)} %bitcast.157, bf16[1024,4096]{1,0:T(8,128)(2,1)} %bitcast.147, f32[640,4096]{1,0:T(8,128)} %get-tuple-element.101, f32[4096]{0:T(1024)S(1)} %fusion.53), kind=kOutput, calls=%fused_computation.17 | convolution fusion | flops 5413269504 | bytes 35946496 | tf_op jit(solution)/shard_map/dot_general | solution.py:398
  271.4 10.4 %multiply_reduce_fusion.1 = (f32[1024]{0:T(1024)S(1)}, f32[640]{0:T(1024)S(1)}, f32[640]{0:T(1024)S(1)}, f32[1024]{0:T(1024)S(1)}, f32[640,1024]{1,0:T(8,128)S(1)}) fusion(f32[640,1024]{1,0:T(8,128)S(1)} %copy-done.11, f32[640]{0:T(1024)S(1)} %add_rsqrt_fusion, f32[640]{0:T(1024)S(1)} %broadcast_multiply_fusion.4, f32[1024]{0:T(1024)S(1)} %reshape.409, ...), kind=kOutput, calls=%fused_computation.55 | convolution fusion | flops 5374604288 | bytes 18896896 | tf_op jit(solution)/shard_map/dot_general | solution.py:398
  284.5 2.6 convolution_convert_fusion.4
  287.1 3.4 reshape.414
  290.4 4.1 copy.77
  294.5 15.3 %multiply_reduce_fusion = (f32[2,16,320]{2,1,0:T(8,128)S(1)}, f32[2,16,320,320]{2,3,1,0:T(8,128)}) fusion(f32[2,16,320,320]{2,3,1,0:T(8,128)} %get-tuple-element.98, f32[2,16,320]{2,1,0:T(8,128)S(1)} %get-tuple-element.97, bf16[2,320,16,64]{1,3,2,0:T(8,128)(2,1)} %copy.77, f32[2,320,16,64]{1,0,3,2:T(2,128)} %reshape_squeeze.11, f32[16,64]{1,0:T(8,128)S(1)} %copy-done.39), kind=kOutput, calls=%fused_computation.2 | convolution fusion | flops 430561280 | bytes 30232576 | tf_op jit(solution)/shard_map/bqhc,bkhc->bhqk/dot_general | solution.py:508
  309.9 11.0 %multiply_convert_fusion = bf16[2,16,320,320]{2,3,1,0:T(8,128)(2,1)S(1)} fusion(f32[2,16,320,320]{2,3,1,0:T(8,128)} %get-tuple-element.104, f32[2,16,320]{2,1,0:T(8,128)S(1)} %get-tuple-element.103, f32[2,16,320,320]{2,3,1,0:T(8,128)} %get-tuple-element.98, f32[2,16,320]{2,1,0:T(8,128)S(1)} %get-tuple-element.97), kind=kLoop, calls=%fused_computation.1 | loop fusion | flops 13107200 | bytes 32849920 | tf_op jit(solution)/shard_map/convert_element_type | solution.py:512
  320.9 1.7 convert_reduce_fusion.2
  323.9 2.8 copy.80
  326.7 4.5 stack_reshape_reshape.9
  331.2 5.7 %fusion.35 = bf16[2,320,16,64]{1,3,2,0:T(8,128)(2,1)S(1)} fusion(bf16[2,16,320,320]{2,3,1,0:T(8,128)(2,1)} %copy-done.6, f32[2,320,16,64]{1,0,3,2:T(2,128)S(1)} %copy-done.9, f32[16,64]{1,0:T(8,128)S(1)} %copy-done.28), kind=kOutput, calls=%fused_computation.81 | convolution fusion | flops 422051840 | bytes 10489856 | tf_op jit(solution)/shard_map/bhqk,bqhc->bkhc/dot_general | solution.py:517
  336.9 1.6 copy.82
  338.5 2.2 stack_reshape_reshape.10
  340.7 8.1 %convert_reduce_fusion.1 = (f32[16,64]{1,0:T(8,128)S(1)}, bf16[2,320,16,64]{1,3,2,0:T(8,128)(2,1)S(1)}) fusion(bf16[2,320,16,64]{1,3,2,0:T(8,128)(2,1)S(1)} %copy-done.20, f32[2,16,320,320]{2,3,1,0:T(8,128)} %get-tuple-element.98, f32[2,16,320]{2,1,0:T(8,128)S(1)} %get-tuple-element.97), kind=kOutput, calls=%fused_computation.48 | convolution fusion | flops 427949056 | bytes 15773696 | tf_op jit(solution)/shard_map/bhqk,bqhc->bkhc/dot_general | solution.py:509
  350.4 2.0 stack_reshape_reshape.11
  352.4 2.0 pad_maximum_fusion
  354.4 2.3 copy.86
  356.9 10.5 %multiply_reduce_fusion.2 = (f32[1024]{0:T(1024)S(1)}, f32[640]{0:T(1024)S(1)}, f32[640]{0:T(1024)S(1)}, f32[1024]{0:T(1024)S(1)}, f32[640,1024]{1,0:T(8,128)}) fusion(bf16[2,320,1024]{2,1,0:T(8,128)(2,1)S(1)} %copy-done.8, f32[640]{0:T(1024)S(1)} %div.43, f32[640]{0:T(1024)S(1)} %rsqrt.22, f32[640]{0:T(1024)S(1)} %copy-done.37, f32[1024]{0:T(1024)S(1)} %copy-done.33, ...), kind=kOutput, calls=%fused_computation.57 | convolution fusion | flops 4033737728 | bytes 14180864 | tf_op jit(solution)/shard_map/dot_general | solution.py:398
  369.2 12.2 %convolution_convert_fusion = bf16[1024,4096]{1,0:T(8,128)(2,1)} fusion(bf16[640,4096]{1,0:T(8,128)(2,1)} %get-tuple-element.111, f32[640,1024]{1,0:T(8,128)} %copy-done.10, f32[1024]{0:T(1024)S(1)} %reshape.410, f32[1024]{0:T(1024)S(1)} %reshape.409, f32[640]{0:T(1024)S(1)} %add_rsqrt_fusion, f32[640]{0:T(1024)S(1)} %broadcast_multiply_fusion.4), kind=kOutput, calls=%fused_computation.36 | convolution fusion | flops 5376180224 | bytes 16266240 | tf_op jit(solution)/shard_map/dot_general | solution.py:398
  381.4 3.1 convolution_convert_fusion.3
  384.6 7.1 %convolution_convert_fusion.2 = bf16[1024,3072]{1,0:T(8,128)(2,1)} fusion(bf16[640,1024]{1,0:T(8,128)(2,1)S(1)} %bitcast.166, bf16[640,3072]{0,1:T(8,128)(2,1)S(1)} %bitcast.160), kind=kOutput, calls=%fused_computation.38 | convolution fusion | flops 4029677568 | bytes 11534336 | tf_op jit(solution)/shard_map/dot_general | solution.py:398
  391.7 9.2 %convolution_convert_fusion.1 = bf16[4096,1024]{0,1:T(8,128)(2,1)} fusion(bf16[640,4096]{1,0:T(8,128)(2,1)S(1)} %bitcast.173, bf16[640,1024]{1,0:T(8,128)(2,1)S(1)} %bitcast.158), kind=kOutput, calls=%fused_computation.37 | convolution fusion | flops 5372903424 | bytes 14942208 | tf_op jit(solution)/shard_map/dot_general | solution.py:398
  400.9 125.9 %fold_grads.1 = (f32[64,1536]{1,0:T(8,128)}, f32[64,512]{1,0:T(8,128)}, f32[64,2048]{1,0:T(8,128)}, f32[64,2048]{1,0:T(8,128)}, f32[8,384]{1,0:T(8,128)}) custom-call(bf16[2,2,2,2,64,3072]{5,4,3,2,1,0:T(8,128)(2,1)} %bitcast.156, bf16[2,2,2,2,64,1024]{5,4,3,2,1,0:T(8,128)(2,1)} %bitcast.162, bf16[2,2,2,2,64,4096]{5,4,3,2,1,0:T(8,128)(2,1)} %bitcast.153, ...), custom_call_target="tpu_custom_call" | custom-call | tf_op jit(solution)/shard_map/fold_grads/pallas_call | solution.py:335
  531.6 4.1 add_multiply_fusion
  535.8 10.9 %add_convert_fusion = bf16[640,1024]{1,0:T(8,128)(2,1)} fusion(f32[640,1024]{1,0:T(8,128)} %copy-done.10, bf16[640,4096]{1,0:T(8,128)(2,1)} %get-tuple-element.75, bf16[1024,4096]{1,0:T(8,128)(2,1)} %bitcast.148, f32[1024]{0:T(1024)S(1)} %reshape.412), kind=kOutput, calls=%fused_computation.63 | convolution fusion | flops 5370675200 | bytes 17567744 | tf_op jit(solution)/shard_map/dot_general | solution.py:398
  (131 shorter events, 24.0 us)
Async XLA Ops:
  0.6 11.6 %copy-start.2 = (bf16[2048,64]{0,1:T(8,128)(2,1)S(1)}, bf16[2048,64]{0,1:T(8,128)(2,1)}, u32[]{:S(2)}) copy-start(bf16[2048,64]{0,1:T(8,128)(2,1)} %param.30) | copy-start | bytes 786436
  0.7 11.6 %copy-start.1 = (bf16[64,2048]{1,0:T(8,128)(2,1)S(1)}, bf16[64,2048]{1,0:T(8,128)(2,1)}, u32[]{:S(2)}) copy-start(bf16[64,2048]{1,0:T(8,128)(2,1)} %refs_2_.1) | copy-start | bytes 786436
  3.3 147.2 %copy-start.30 = (f32[2,320]{1,0:T(2,128)}, f32[2,320]{1,0:T(2,128)S(1)}, u32[]{:S(2)}) copy-start(f32[2,320]{1,0:T(2,128)S(1)} %broadcast_multiply_fusion.5) | copy-start | bytes 7684
  5.2 145.3 %copy-start.34 = (f32[2,320]{1,0:T(2,128)}, f32[2,320]{1,0:T(2,128)S(1)}, u32[]{:S(2)}) copy-start(f32[2,320]{1,0:T(2,128)S(1)} %add_rsqrt_fusion.1) | copy-start | bytes 7684
  12.3 0.8 copy-start.3
  129.1 2.6 copy-start
  131.7 3.3 copy-start.4
  135.0 3.3 copy-start.5
  139.3 11.2 %copy-start.32 = (f32[1024]{0:T(1024)}, f32[1024]{0:T(1024)S(1)}, u32[]{:S(2)}) copy-start(f32[1024]{0:T(1024)S(1)} %reshape.404) | copy-start | bytes 12292
  141.3 9.2 %copy-start.21 = (bf16[2,320,1024]{2,1,0:T(8,128)(2,1)}, bf16[2,320,1024]{2,1,0:T(8,128)(2,1)S(1)}, u32[]{:S(2)}) copy-start(bf16[2,320,1024]{2,1,0:T(8,128)(2,1)S(1)} %add_convert_fusion.2) | copy-start | bytes 3932164
  157.1 4.6 copy-start.15
  178.3 11.8 %copy-start.27 = (f32[16,64]{1,0:T(8,128)}, f32[16,64]{1,0:T(8,128)S(1)}, u32[]{:S(2)}) copy-start(f32[16,64]{1,0:T(8,128)S(1)} %reshape.407) | copy-start | bytes 12292
  198.6 0.6 copy-start.38
  207.3 7.5 %copy-start.7 = (bf16[2,320,1024]{2,1,0:T(8,128)(2,1)S(1)}, bf16[2,320,1024]{2,1,0:T(8,128)(2,1)}, u32[]{:S(2)}) copy-start(bf16[2,320,1024]{2,1,0:T(8,128)(2,1)} %param.16) | copy-start | bytes 3932164
  214.9 3.3 copy-start.36
  218.2 1.5 copy-start.10
  220.2 33.9 %copy-start.16 = (bf16[2,320,1024]{2,1,0:T(8,128)(2,1)S(1)}, bf16[2,320,1024]{2,1,0:T(8,128)(2,1)}, u32[]{:S(2)}) copy-start(bf16[2,320,1024]{2,1,0:T(8,128)(2,1)} %param.18) | copy-start | bytes 3932164
  254.1 17.4 %copy-start.11 = (f32[640,1024]{1,0:T(8,128)S(1)}, f32[640,1024]{1,0:T(8,128)}, u32[]{:S(2)}) copy-start(f32[640,1024]{1,0:T(8,128)} %copy-done.10) | copy-start | bytes 7864324
  283.0 1.5 copy-start.12
  287.1 7.5 %copy-start.39 = (f32[16,64]{1,0:T(8,128)S(1)}, f32[16,64]{1,0:T(8,128)}, u32[]{:S(2)}) copy-start(f32[16,64]{1,0:T(8,128)} %copy-done.38) | copy-start | bytes 12292
  309.9 11.0 %copy-start.14 = (bf16[2,320,16,64]{1,0,3,2:T(2,128)(2,1)S(1)}, bf16[2,320,16,64]{1,0,3,2:T(2,128)(2,1)}, u32[]{:S(2)}) copy-start(bf16[2,320,16,64]{1,0,3,2:T(2,128)(2,1)} %convert_element_type.239) | copy-start | bytes 3932164
  320.8 3.1 copy-start.6
  323.9 7.2 %copy-start.9 = (f32[2,320,16,64]{1,0,3,2:T(2,128)S(1)}, f32[2,320,16,64]{1,0,3,2:T(2,128)}, u32[]{:S(2)}) copy-start(f32[2,320,16,64]{1,0,3,2:T(2,128)} %reshape_squeeze.12) | copy-start | bytes 7864324
  323.9 7.2 %copy-start.28 = (f32[16,64]{1,0:T(8,128)S(1)}, f32[16,64]{1,0:T(8,128)}, u32[]{:S(2)}) copy-start(f32[16,64]{1,0:T(8,128)} %copy-done.27) | copy-start | bytes 12292
  336.9 3.8 copy-start.20
  348.8 3.6 copy-start.18
  354.4 2.4 copy-start.35
  354.4 2.4 copy-start.31
  354.4 2.5 copy-start.8
  354.4 2.5 copy-start.33
  354.4 2.5 copy-start.37
  356.9 11.0 %copy-start.17 = (bf16[2,320,1024]{2,1,0:T(8,128)(2,1)S(1)}, bf16[2,320,1024]{2,1,0:T(8,128)(2,1)}, u32[]{:S(2)}) copy-start(bf16[2,320,1024]{2,1,0:T(8,128)(2,1)} %param.18) | copy-start | bytes 3932164
  369.2 12.2 %copy-start.13 = (f32[640,1024]{1,0:T(8,128)S(1)}, f32[640,1024]{1,0:T(8,128)}, u32[]{:S(2)}) copy-start(f32[640,1024]{1,0:T(8,128)} %copy-done.12) | copy-start | bytes 7864324
  369.2 12.2 %copy-start.23 = (bf16[640,1024]{0,1:T(8,128)(2,1)S(1)}, bf16[640,1024]{0,1:T(8,128)(2,1)}, u32[]{:S(2)}) copy-start(bf16[640,1024]{0,1:T(8,128)(2,1)} %reshape.378) | copy-start | bytes 3932164
  381.4 3.2 copy-start.19
  381.4 3.2 copy-start.22
  381.4 10.3 %slice-start = ((s8[5242880]{0:T(1024)(128)(4,1)}), s8[1048576]{0:T(1024)(128)(4,1)S(1)}, s32[]{:S(2)}) async-start(s8[5242880]{0:T(1024)(128)(4,1)} %bitcast.172), calls=%async_computation | async-start | bytes 2097152
  384.6 7.1 %slice-start.1 = ((s8[5242880]{0:T(1024)(128)(4,1)}), s8[4194304]{0:T(1024)(128)(4,1)S(1)}, s32[]{:S(2)}) async-start(s8[5242880]{0:T(1024)(128)(4,1)} %bitcast.172), calls=%async_computation.1 | async-start | bytes 8388608
  531.6 4.1 copy-start.29
  535.8 10.9 %copy-start.26 = (f32[64,512]{1,0:T(8,128)S(1)}, f32[64,512]{1,0:T(8,128)}, u32[]{:S(2)}) copy-start(f32[64,512]{1,0:T(8,128)} %get-tuple-element.32) | copy-start | bytes 393220
  535.8 11.6 %copy-start.25 = (f32[64,2048]{1,0:T(8,128)S(1)}, f32[64,2048]{1,0:T(8,128)}, u32[]{:S(2)}) copy-start(f32[64,2048]{1,0:T(8,128)} %get-tuple-element.140) | copy-start | bytes 1572868
  535.8 12.4 %copy-start.24 = (f32[64,2048]{1,0:T(8,128)S(1)}, f32[64,2048]{1,0:T(8,128)}, u32[]{:S(2)}) copy-start(f32[64,2048]{1,0:T(8,128)} %get-tuple-element.34) | copy-start | bytes 1572868

commit v3 on v1

v3 whole, which is shorter than its diff:
```python
import functools
import math

import jax
import jax.numpy as jnp
from jax import lax
from jax.experimental import pallas as pl
from jax.experimental.pallas import tpu as pltpu
from jax.sharding import PartitionSpec as P

HEAD_DIM = 64
EPSILON = 1e-06
BOTH = ("dp", "tensor")
MESH = pl.DeviceIdType.MESH
LANES = 128
bf16 = jnp.bfloat16
f32 = jnp.float32
NN = ((1,), (0,))
NT = ((1,), (1,))
TN = ((0,), (0,))


def mm(a, b, dims):
    return lax.dot_general(a, b, (dims, ((), ())), preferred_element_type=f32)


class Place:
    def __init__(self, dp_count):
        self.bits = int(math.log2(dp_count))
        self.dp = lax.axis_index("dp")
        self.tensor = lax.axis_index("tensor")
        self.own = [lax.rem(lax.div(self.dp, 2**k), 2) for k in range(self.bits)]

    def partner(self, stage):
        if stage == "t":
            return {"tensor": 1 - self.tensor}
        return {"dp": self.dp + (1 - 2 * self.own[stage]) * 2**stage}

    def greet(self):
        barrier = pltpu.get_barrier_semaphore()
        stages = list(range(self.bits)) + ["t"]
        for stage in stages:
            pl.semaphore_signal(barrier, inc=1, device_id=self.partner(stage), device_id_type=MESH)
        pl.semaphore_wait(barrier, len(stages))

    def lead(self, done, flipped=None):
        index = []
        for bit in range(self.bits - 1, -1, -1):
            if bit in done:
                index.append(slice(None))
            elif bit == flipped:
                index.append(1 - self.own[bit])
            else:
                index.append(self.own[bit])
        return tuple(index)


def stage_orders(bits):
    far = list(range(bits - 1, 1, -1))
    return (far + [1, "t"], far + ["t", 1], [1] + far + ["t"], ["t"] + far + [1])


class Flow:
    def __init__(self, entry, bits):
        self.matrix, self.first, self.count, which, self.start = entry
        self.order = stage_orders(bits)[which]
        self.stages = len(self.order)

    def remote(self, src, dst, stage, slot):
        return pltpu.make_async_remote_copy(
            src_ref=src,
            dst_ref=dst,
            send_sem=self.send.at[slot],
            recv_sem=self.recv.at[slot],
            device_id=self.place.partner(stage),
            device_id_type=MESH,
        )


class Spread(Flow):
    def __init__(self, entry, bits, base):
        super().__init__(entry, bits)
        self.plane_slot, self.across_slot = [], [base]
        slot, twice = base + 1, 1
        for stage in self.order:
            self.plane_slot.append(slot)
            self.across_slot.append(slot + twice)
            slot += 2 * twice
            if stage == "t":
                twice = 2
        self.end = slot

    def bind(self, place, shard, full, half, send, recv, local):
        self.place, self.shard, self.full, self.half = place, shard, full, half
        self.send, self.recv, self.local = send, recv, local

    def views(self, done, flipped=None):
        place = self.place
        if "t" in done:
            sides = [0, 1]
        elif flipped == "t":
            sides = [1 - place.tensor]
        else:
            sides = [place.tensor]
        lead = place.lead(done, flipped)
        found = []
        for side in sides:
            start = pl.multiple_of(side * self.half + self.first, LANES)
            found.append(self.full.at[lead + (slice(None), pl.ds(start, self.count))])
        return found

    def piece(self):
        return self.shard.at[:, pl.ds(self.first, self.count)]

    def keep(self):
        return pltpu.make_async_copy(self.piece(), self.views(set())[0], self.local)

    def plane(self, step):
        targets = self.views(set(self.order[:step]))
        sources = [self.piece()] if step == 0 else targets
        slot = self.plane_slot[step]
        return [
            self.remote(src, dst, self.order[step], slot + i)
            for i, (src, dst) in enumerate(zip(sources, targets))
        ]

    def across(self, step):
        slot = self.across_slot[step]
        if step == 0:
            return [self.remote(self.piece(), self.views(set())[0], 0, slot)]
        fresh = self.views(set(self.order[: step - 1]), self.order[step - 1])
        return [self.remote(view, view, 0, slot + i) for i, view in enumerate(fresh)]

    def tick(self, step):
        if step == 0:
            self.keep().start()
        else:
            for made in self.plane(step - 1):
                made.wait_recv()
        if step == 1:
            self.keep().wait()
        if step < self.stages:
            for made in self.plane(step):
                made.start()
        for made in self.across(step):
            made.start()

    def finish(self):
        for step in range(self.stages):
            for made in self.plane(step):
                made.wait_send()
        for step in range(self.stages + 1):
            for made in self.across(step):
                made.wait()


class Fold(Flow):
    def __init__(self, entry, bits, base):
        super().__init__(entry, bits)
        self.order = list(reversed(self.order))
        self.base = base
        self.end = base + 2 + self.stages

    def bind(self, place, partial, half, total, landing, result, send, recv, local):
        self.place, self.partial, self.half = place, partial, half
        self.total, self.landing, self.result = total, landing, result
        self.send, self.recv, self.local = send, recv, local

    def loads(self):
        every = set(range(1, self.place.bits))
        made = []
        for side in (0, 1):
            columns = pl.ds(side * self.half + self.first, self.count)
            mine = self.partial.at[self.place.lead(every) + (slice(None), columns)]
            made.append(pltpu.make_async_copy(mine, self.total.at[side], self.local.at[side]))
        return made

    def cores(self):
        every = set(range(1, self.place.bits))
        made = []
        for side in (0, 1):
            columns = pl.ds(side * self.half + self.first, self.count)
            theirs = self.partial.at[self.place.lead(every, 0) + (slice(None), columns)]
            made.append(self.remote(theirs, self.landing[0].at[side], 0, self.base + side))
        return made

    def begin(self):
        for made in self.loads() + self.cores():
            made.start()

    def where(self, done, last=None):
        place = self.place
        index = []
        for name in ["t"] + list(range(place.bits - 1, 0, -1)):
            own = place.tensor if name == "t" else place.own[name]
            if name in done:
                index.append(own)
            elif name == last:
                index.append(1 - own)
            else:
                index.append(None)
        return index

    def stage(self, step):
        index = self.where(set(self.order[:step]), self.order[step])
        view = self.total.at[tuple(slice(None) if e is None else e for e in index)]
        return self.remote(view, self.landing[step + 1], self.order[step], self.base + 2 + step)

    def add(self, landing, done):
        index = self.where(done)
        free = [i for i, entry in enumerate(index) if entry is None]

        def one(j, carry):
            spots, inner = list(index), []
            for position, dim in enumerate(free):
                bit = lax.rem(lax.div(j, 2 ** (len(free) - 1 - position)), 2)
                spots[dim] = bit
                inner.append(bit)
            spots, inner = tuple(spots), tuple(inner)
            value = self.total[spots].astype(f32) + landing[inner].astype(f32)
            self.total[spots] = value.astype(self.total.dtype)
            return carry

        lax.fori_loop(0, 2 ** len(free), one, 0)

    def tick(self, step):
        order = self.order
        if step == 0:
            for made in self.loads():
                made.wait()
            for made in self.cores():
                made.wait_recv()
            self.add(self.landing[0], set())
        else:
            self.stage(step - 1).wait_recv()
            if step < self.stages:
                self.add(self.landing[step], set(order[:step]))
            else:
                spots = tuple(self.where(set(order)))
                value = self.total[spots].astype(f32) + self.landing[step][...].astype(f32)
                self.result[:, self.first : self.first + self.count] = value
        if step < self.stages:
            self.stage(step).start()

    def finish(self):
        for made in self.cores():
            made.wait_send()
        for step in range(self.stages):
            self.stage(step).wait_send()


def fold_scratch(bits, rows, count, dtype):
    lead = (2,) * bits
    shapes = [pltpu.VMEM(lead + (rows, count), dtype)]
    for stage in range(bits + 1):
        shapes.append(pltpu.VMEM(lead[stage:] + (rows, count), dtype))
    return shapes


class Travel:
    def __init__(self, kind, arrays, plan, dp_count):
        self.kind, self.dp_count = kind, dp_count
        self.bits = int(math.log2(dp_count))
        self.flows, base = [], 0
        for entry in plan:
            flow = kind(entry, self.bits, base)
            base = flow.end
            self.flows.append(flow)
        self.count = len(arrays)
        self.ticks = max(flow.start + flow.stages for flow in self.flows) + 1
        any_space = pl.BlockSpec(memory_space=pl.ANY)
        lead = (2,) * self.bits
        self.scratch = [pltpu.SemaphoreType.DMA((base,)), pltpu.SemaphoreType.DMA((base,))]
        if kind is Spread:
            self.operands = list(arrays)
            self.halves = [a.shape[1] for a in arrays]
            self.in_specs = [any_space] * self.count
            self.out_shape = [
                jax.ShapeDtypeStruct(lead + (a.shape[0], 2 * a.shape[1]), a.dtype) for a in arrays
            ]
            self.out_specs = [any_space] * self.count
            self.scratch.append(pltpu.SemaphoreType.DMA((len(plan) + self.count,)))
            self.scratch += [pltpu.VMEM(a.shape, a.dtype) for a in arrays]
        else:
            self.operands = [
                a.reshape(lead + (a.shape[0] // dp_count, a.shape[1])) for a in arrays
            ]
            self.halves = [a.shape[1] // 2 for a in arrays]
            rows = [a.shape[0] // dp_count for a in arrays]
            self.in_specs = [any_space] * self.count
            self.out_shape = [
                jax.ShapeDtypeStruct((r, h), f32) for r, h in zip(rows, self.halves)
            ]
            self.out_specs = [
                pl.BlockSpec((r, h), lambda *g: (0, 0)) for r, h in zip(rows, self.halves)
            ]
            self.scratch.append(pltpu.SemaphoreType.DMA((len(plan), 2)))
            for flow in self.flows:
                a = arrays[flow.matrix]
                self.scratch += fold_scratch(self.bits, rows[flow.matrix], flow.count, a.dtype)

    def bind(self, sources, targets, scratch):
        self.place = Place(self.dp_count)
        send, recv, local = scratch[:3]
        self.local, self.sources, self.held = local, sources, scratch[3:]
        each = self.bits + 2
        for i, flow in enumerate(self.flows):
            m = flow.matrix
            if self.kind is Spread:
                flow.bind(
                    self.place, self.held[m], targets[m], self.halves[m], send, recv, local.at[i]
                )
            else:
                mine = self.held[i * each : (i + 1) * each]
                flow.bind(
                    self.place,
                    sources[m],
                    self.halves[m],
                    mine[0],
                    mine[1:],
                    targets[m],
                    send,
                    recv,
                    local.at[i],
                )

    def begin(self):
        self.place.greet()
        if self.kind is Spread:
            loads = [
                pltpu.make_async_copy(src, dst, self.local.at[len(self.flows) + i])
                for i, (src, dst) in enumerate(zip(self.sources, self.held))
            ]
            for made in loads:
                made.start()
            for made in loads:
                made.wait()
        else:
            for flow in self.flows:
                flow.begin()

    def tick(self, number):
        for flow in self.flows:
            if 0 <= number - flow.start <= flow.stages:
                flow.tick(number - flow.start)

    def finish(self):
        for flow in self.flows:
            flow.finish()

    def results(self, outs):
        if self.kind is Spread:
            return [o.reshape(-1, o.shape[-1]) for o in outs]
        return list(outs)


def carried_kernel(travel, compute, points, steps, ins, outs, *refs):
    n = travel.count
    here = refs[:ins]
    sources = refs[ins : ins + n]
    made = refs[ins + n : ins + n + outs]
    targets = refs[ins + n + outs : ins + 2 * n + outs]
    scratch = refs[ins + 2 * n + outs :]
    travel.bind(sources, targets, scratch[: len(travel.scratch)])
    total = points * steps
    due = {}
    for number in range(travel.ticks):
        due.setdefault(min(number * total // travel.ticks, total - 1), []).append(number)

    def at(point):
        for step in range(steps):
            numbers = due.get(step * points + point, [])
            first = step == 0 and point == 0
            if not numbers and not first:
                continue

            def act(numbers=numbers, first=first):
                if first:
                    travel.begin()
                for number in numbers:
                    travel.tick(number)

            if steps == 1:
                act()
            else:
                pl.when(pl.program_id(0) == step)(act)

    compute(*here, *made, *scratch[len(travel.scratch) :], at)
    if steps == 1:
        travel.finish()
    else:
        pl.when(pl.program_id(0) == steps - 1)(travel.finish)


def carry(travel, collective, name, compute=None, points=1, steps=1, operands=(), in_specs=(),
          out_shape=(), out_specs=(), scratch=(), flops=0, vmem=60):
    if compute is None:

        def compute(at):
            for point in range(points):
                at(point)

    outs = pl.pallas_call(
        functools.partial(
            carried_kernel, travel, compute, points, steps, len(operands), len(out_shape)
        ),
        grid=() if steps == 1 else (steps,),
        out_shape=list(out_shape) + travel.out_shape,
        in_specs=list(in_specs) + travel.in_specs,
        out_specs=list(out_specs) + travel.out_specs,
        scratch_shapes=travel.scratch + list(scratch),
        compiler_params=pltpu.CompilerParams(
            collective_id=collective, has_side_effects=True, vmem_limit_bytes=vmem << 20
        ),
        name=name,
    )(*operands, *travel.operands)
    return list(outs[: len(out_shape)]), travel.results(outs[len(out_shape) :])


def make_plan(sizes, fractions):
    plan, position, tick = [], {}, 0
    for matrix, size in sizes:
        start = position.get(matrix, 0)
        units, total, taken, gone = size // LANES, sum(fractions), 0, 0
        for which, weight in enumerate(fractions):
            taken += weight
            upto = (units * taken * 2 + total) // (2 * total)
            if upto > gone:
                plan.append((matrix, start + gone * LANES, (upto - gone) * LANES, which, tick))
            gone = upto
        position[matrix] = start + size
        tick += 1
    return plan


EVEN = (1, 1, 1, 1)


def chunks(order, halves):
    sizes = []
    for matrix in order:
        half = halves[matrix]
        if half > 1536:
            sizes += [(matrix, half // 2)] * 2
        else:
            sizes.append((matrix, half))
    return sizes


def softmax_rows(scores, valid):
    scores = jnp.where(valid > 0.5, scores, -1000000000.0)
    shifted = jnp.exp(scores - jnp.max(scores, axis=-1, keepdims=True))
    return shifted * (1.0 / jnp.sum(shifted, axis=-1, keepdims=True))


def head_masks():
    lane = lax.broadcasted_iota(jnp.int32, (1, LANES), 1)
    per = LANES // HEAD_DIM
    return [(lane // HEAD_DIM == h).astype(f32).astype(bf16) for h in range(per)], lane


def pick(parts, lane):
    out = parts[0]
    for h in range(1, len(parts)):
        out = jnp.where(lane // HEAD_DIM == h, parts[h], out)
    return out


def attend(first, wq, wk, wv, qb, vb, valid, q_out, k_out, v_out, mix_out, at):
    images, slots = valid.shape[0], valid.shape[2]
    at(0)
    q_out[...] = (mm(first[...], wq[...], NN) + qb[...]).astype(bf16)
    k_out[...] = mm(first[...], wk[...], NN).astype(bf16)
    at(1)
    v_out[...] = (mm(first[...], wv[...], NN) + vb[...]).astype(bf16)
    at(2)
    masks, lane = head_masks()
    point = 3
    for image in range(images):
        rows = slice(image * slots, (image + 1) * slots)
        for pair in range(q_out.shape[1] // LANES):
            columns = slice(pair * LANES, (pair + 1) * LANES)
            query = q_out[rows, columns] * bf16(HEAD_DIM**-0.5)
            key, value = k_out[rows, columns], v_out[rows, columns]
            parts = []
            for mask in masks:
                probs = softmax_rows(mm(query, key * mask, NT), valid[image])
                parts.append(mm(probs.astype(bf16), value, NN))
            mix_out[rows, columns] = pick(parts, lane).astype(bf16)
            at(point)
            point += 1


def attend_back(q, k, v, mixed, grad_attn, grad_attn_t, first_t, out_t, wq, wk, wv, valid,
                out_part, q_part, k_part, v_part, grad_first, qb_grad, vb_grad,
                gm, dq, dk, dv, at):
    images, slots = valid.shape[0], valid.shape[2]
    scale = HEAD_DIM**-0.5
    at(0)
    gm[...] = mm(grad_attn[...], out_t[...], NN).astype(bf16)
    out_part[...] = mm(grad_attn_t[...], mixed[...], NN).astype(bf16)
    at(1)
    masks, lane = head_masks()
    point = 2
    for image in range(images):
        rows = slice(image * slots, (image + 1) * slots)
        for pair in range(q.shape[1] // LANES):
            columns = slice(pair * LANES, (pair + 1) * LANES)
            query = q[rows, columns] * bf16(scale)
            key, value, grad = k[rows, columns], v[rows, columns], gm[rows, columns]
            dqs, dks, dvs = [], [], []
            for mask in masks:
                probs = softmax_rows(mm(query, key * mask, NT), valid[image])
                pulled = mm(grad, value * mask, NT)
                dvs.append(mm(probs.astype(bf16), grad, TN))
                inner = jnp.sum(probs * pulled, axis=-1, keepdims=True)
                grad_scores = (probs * (pulled - inner)).astype(bf16)
                dqs.append(mm(grad_scores, key, NN))
                dks.append(mm(grad_scores, query, TN))
            dq[rows, columns] = (pick(dqs, lane) * scale).astype(bf16)
            dk[rows, columns] = pick(dks, lane).astype(bf16)
            dv[rows, columns] = pick(dvs, lane).astype(bf16)
            at(point)
            point += 1
    qb_grad[...] = jnp.sum(dq[...].astype(f32), axis=0, keepdims=True)
    vb_grad[...] = jnp.sum(dv[...].astype(f32), axis=0, keepdims=True)
    q_part[...] = mm(first_t[...], dq[...], NN).astype(bf16)
    k_part[...] = mm(first_t[...], dk[...], NN).astype(bf16)
    at(point)
    v_part[...] = mm(first_t[...], dv[...], NN).astype(bf16)
    back = mm(dq[...], wq[...], NT) + mm(dk[...], wk[...], NT) + mm(dv[...], wv[...], NT)
    at(point + 1)

    @pl.when(pl.program_id(0) == 0)
    def _():
        grad_first[...] = back

    @pl.when(pl.program_id(0) > 0)
    def _():
        grad_first[...] += back


WIDE = 2 * LANES


def whole(shape):
    return pl.BlockSpec(shape, lambda p: (0,) * len(shape), pipeline_mode=pl.Buffered(1))


def across(rows):
    return pl.BlockSpec((rows, WIDE), lambda p: (0, p))


def attention(travel, collective, first, weights, qbias, vbias, valid):
    tokens, width = first.shape
    shape = jax.ShapeDtypeStruct((tokens, width), bf16)
    images = valid.shape[0]
    return carry(
        travel,
        collective,
        "attention",
        compute=attend,
        points=3 + images * (WIDE // LANES),
        steps=width // WIDE,
        operands=(first, *weights, qbias.reshape(1, -1), vbias.reshape(1, -1), valid),
        in_specs=(
            [whole((tokens, width))]
            + [across(width)] * 3
            + [across(1)] * 2
            + [whole(valid.shape)]
        ),
        out_shape=[shape] * 4,
        out_specs=[across(tokens)] * 4,
    )


def attention_back(travel, collective, q, k, v, mixed, grad_attn, first, out_t, weights, valid):
    tokens, width = first.shape
    images = valid.shape[0]
    part = jax.ShapeDtypeStruct((width, width), bf16)
    vector = jax.ShapeDtypeStruct((1, width), f32)
    return carry(
        travel,
        collective,
        "attention_back",
        compute=attend_back,
        points=4 + images * (WIDE // LANES),
        steps=width // WIDE,
        operands=(q, k, v, mixed, grad_attn, grad_attn.T, first.T, out_t, *weights, valid),
        in_specs=(
            [across(tokens)] * 4
            + [whole((tokens, width)), whole((width, tokens)), whole((width, tokens))]
            + [across(width)] * 4
            + [whole(valid.shape)]
        ),
        out_shape=[part] * 4 + [jax.ShapeDtypeStruct((tokens, width), f32)] + [vector] * 2,
        out_specs=(
            [across(width)] * 4 + [whole((tokens, width))] + [across(1)] * 2
        ),
        scratch=[pltpu.VMEM((tokens, WIDE), bf16)] * 4,
    )


def exact_gelu(values):
    return jax.nn.gelu(values, approximate=False)


def norm_stats(values):
    average = jnp.mean(values, axis=-1, keepdims=True)
    centered = values - average
    variance = jnp.mean(centered * centered, axis=-1, keepdims=True)
    scale = lax.rsqrt(variance + EPSILON)
    return centered * scale, scale


def norm_back(grad, unit, scale, gain):
    z = grad * gain
    mean_z = jnp.mean(z, axis=-1, keepdims=True)
    mean_zx = jnp.mean(z * unit, axis=-1, keepdims=True)
    return scale * (z - mean_z - unit * mean_zx)


def total(values):
    return jnp.sum(values.astype(f32), axis=0)


def shards(
    inputs,
    lengths,
    cotangent,
    first_gain,
    first_shift,
    qkv_weight,
    query_bias,
    value_bias,
    out_weight,
    out_bias,
    second_gain,
    second_shift,
    up_weight,
    up_bias,
    down_weight,
    down_bias,
):
    image_count, slot_count, width = inputs.shape
    tensor_rank = lax.axis_index("tensor")
    tokens = image_count * slot_count
    dp_count = lax.axis_size("dp")
    device_count = dp_count * lax.axis_size("tensor")

    vectors = (
        first_gain,
        first_shift,
        query_bias,
        value_bias,
        out_bias,
        second_gain,
        second_shift,
        down_bias,
        up_bias,
    )
    sizes = [v.shape[0] for v in vectors]
    packed = jnp.concatenate(vectors)
    length = -(-packed.shape[0] // LANES) * LANES
    packed = jnp.pad(packed, (0, length - packed.shape[0]))
    packed = jnp.broadcast_to(packed, (8, length))

    sources = [qkv_weight[0], qkv_weight[1], qkv_weight[2], packed]
    half = qkv_weight.shape[2]
    plan = [(3, 0, length, 2, 0)] + head_plan(half)
    _, (query_w, key_w, value_w, spread) = carry(
        Travel(Spread, sources, plan, dp_count), 1, "spread_first", points=len(plan) + 8
    )
    spread = spread.reshape(dp_count, 8, 2, length)[:, 0].reshape(device_count, length)
    full = []
    start = 0
    for size in sizes:
        full.append(spread[:, start : start + size].reshape(-1).astype(f32))
        start += size
    gain_one, shift_one, qbias, vbias, obias, gain_two, shift_two, dbias, ubias = full

    positions = jnp.arange(slot_count, dtype=jnp.int32)
    own_lengths = lax.dynamic_slice_in_dim(lengths, tensor_rank * image_count, image_count)
    valid = (positions[None, :] < own_lengths[:, None]).astype(f32)
    valid_rows = valid.reshape(tokens, 1)
    masked = inputs.reshape(tokens, width).astype(f32) * valid_rows
    unit_one, scale_one = norm_stats(masked)
    first = (unit_one * gain_one + shift_one).astype(bf16)

    sources = [out_weight.T, up_weight, down_weight.T]
    halves = [s.shape[1] for s in sources]
    plan = make_plan(chunks((0, 1, 2), halves), EVEN)
    valid = valid.reshape(image_count, 1, slot_count)
    qkv_w = (query_w, key_w, value_w)
    (query, key, value, mixed), (out_t, up_w, down_t) = attention(
        Travel(Spread, sources, plan, dp_count), 2, first, qkv_w, qbias, vbias, valid
    )
    middle = masked + mm(mixed, out_t, NT) + obias
    unit_two, scale_two = norm_stats(middle)
    second = (unit_two * gain_two + shift_two).astype(bf16)
    hidden = mm(second, up_w, NN) + ubias
    active = exact_gelu(hidden).astype(bf16)
    output = (middle + mm(active, down_t, NT) + dbias).astype(bf16)

    grad_low = cotangent.reshape(tokens, width)
    grad_out = grad_low.astype(f32)
    down_part = mm(grad_low, active, TN).astype(bf16)
    grad_active = mm(grad_low, down_t, NN)
    grad_hidden = jax.vjp(exact_gelu, hidden)[1](grad_active)[0].astype(bf16)
    up_part = mm(second, grad_hidden, TN).astype(bf16)
    grad_second = mm(grad_hidden, up_w, NT)
    grad_middle = grad_out + norm_back(grad_second, unit_two, scale_two, gain_two)
    grad_attn = grad_middle.astype(bf16)

    sources = [down_part, up_part]
    halves = [s.shape[1] // 2 for s in sources]
    plan = make_plan(chunks((0, 1), halves), EVEN)
    (out_part, q_part, k_part, v_part, grad_first, qb_grad, vb_grad), (down_grad, up_grad) = (
        attention_back(
            Travel(Fold, sources, plan, dp_count),
            3,
            query,
            key,
            value,
            mixed,
            grad_attn,
            first,
            out_t,
            qkv_w,
            valid,
        )
    )
    grad_in = norm_back(grad_first, unit_one, scale_one, gain_one)
    input_grad = (grad_middle + grad_in) * valid_rows

    vector_grads = (
        total(grad_first * unit_one),
        total(grad_first),
        qb_grad,
        vb_grad,
        total(grad_attn),
        total(grad_second * unit_two),
        total(grad_second),
        total(grad_low),
        total(grad_hidden),
    )
    stacked = jnp.concatenate([v.reshape(device_count, -1) for v in vector_grads], axis=1)
    stacked = jnp.pad(stacked, ((0, 0), (0, length - stacked.shape[1])))
    stacked = stacked.reshape(-1, 1, 2 * length)
    stacked = jnp.pad(stacked, ((0, 0), (0, 7), (0, 0))).reshape(-1, 2 * length)
    sources = [q_part, k_part, v_part, stacked, out_part]
    plan = make_plan([(4, half)], EVEN) + head_plan(half, 1) + [(3, 0, length, 2, 2)]
    _, (q_grad, k_grad, v_grad, own, out_grad) = carry(
        Travel(Fold, sources, plan, dp_count), 4, "fold_last", points=10
    )
    own = own[0]
    shares = []
    start = 0
    for size in sizes:
        shares.append(own[start : start + size])
        start += size

    return (
        output.reshape(inputs.shape),
        input_grad.reshape(inputs.shape),
        shares[0],
        shares[1],
        jnp.stack([q_grad, k_grad, v_grad]),
        shares[2],
        shares[3],
        out_grad.T,
        shares[4],
        shares[5],
        shares[6],
        up_grad,
        shares[8],
        down_grad.T,
        shares[7],
    )


def head_plan(half, start=0):
    plan = []
    for matrix, shares in ((0, (1, 1, 0, 0)), (1, (0, 0, 1, 1)), (2, EVEN)):
        for entry in make_plan([(matrix, half)], shares):
            plan.append(entry[:4] + (start + matrix // 2,))
    return plan


def solution(mesh):
    rows = P(BOTH, None, None)
    vector = P(BOTH)
    return jax.shard_map(
        shards,
        mesh=mesh,
        in_specs=(
            rows,
            P("dp"),
            rows,
            vector,
            vector,
            P(None, "dp", "tensor"),
            vector,
            vector,
            P("tensor", "dp"),
            vector,
            vector,
            vector,
            P("dp", "tensor"),
            vector,
            P("tensor", "dp"),
            vector,
        ),
        out_specs=(
            rows,
            rows,
            vector,
            vector,
            P(None, "dp", "tensor"),
            vector,
            vector,
            P("tensor", "dp"),
            vector,
            vector,
            vector,
            P("dp", "tensor"),
            vector,
            P("tensor", "dp"),
            vector,
        ),
        check_vma=False,
    )
```

time: 1270 us -> 468 us (0.37)
  waiting for transfers between devices: 798 us -> 0 us
  Pallas kernels: 0 us -> 290 us
  blocking collectives: 146 us -> 0 us
  matrix products: 174 us -> 101 us
  local copies, waits for them, and re-layouts: 77 us -> 42.6 us
  other arithmetic: 55.1 us -> 29.2 us
  between operations: 15.1 us -> 1.07 us
    reduce_scatter x6 -> x0, waiting for transfers between devices: 664 us -> none  [scatter_matrix(): lax.psum_scatter(halves, ('tensor', 'dp'), scatter_dimension=0, tiled=True)]
    pallas_call x0 -> x4, Pallas kernels: none -> 290 us  [carry(): pl.pallas_call(functools.partial(carried_kernel, travel, compute, points,...]
    all_gather x6 -> x0, waiting for transfers between devices: 133 us -> none  [gather_matrix(): return lax.all_gather(wide, 'dp', axis=0, tiled=True)]
    all_gather x7 -> x0, blocking collectives: 106 us -> none  [the longest x1 65.8 us: shards(): packed = lax.all_gather(jnp.concatenate(vectors), BOTH, axis=0)]
    reshape x12 -> x2, local copies, waits for them, and re-layouts: 52.6 us -> 2.68 us  [the longest x1 2.63 us: shards(): grad_low = cotangent.reshape(tokens, width)]
    unnamed x1 -> x0, blocking collectives: 39.7 us -> none
    dot_general x5 -> x0, matrix products: 38.4 us -> none  [the longest x1 14.3 us: shards(): jnp.einsum('bqhc,bkhc->bhqk', grad_mixed, value, preferred_element_type=f32)]
    convert_element_type x8 -> x4, other arithmetic: 27 us -> 0.81 us  [the longest x2 0.72 us: shards(): valid = (positions[None, :] < own_lengths[:, None]).astype(f32)]
  transfers between devices with their start and end apart: 12 -> 0, of which waited for: 8 -> 0; matrix products, arithmetic and copies ran while one was open for 18% -> 0% of each run, Pallas kernels for 0% -> 0%
where the time goes in v3:
time: 468 us; the launch traced here: 465 us
  Pallas kernels  290 us (62%)
  matrix products  101 us (22%)
  local copies, waits for them, and re-layouts  42.6 us (9%)
  other arithmetic  29.2 us (6%)
    pallas_call x4, Pallas kernels, carry(): pl.pallas_call(functools.partial(carried_kernel, travel, compute, points,...  290 us
    dot_general x7, matrix products, mm(): return lax.dot_general(a, b, (dims, ((), ())), preferred_element_type=f32)  101 us
    reduce_sum x5, other arithmetic, total(): return jnp.sum(values.astype(f32), axis=0)  12.9 us

profile of v3, /device:TPU:0, one launch (start us, length us, event | category | flops | bytes accessed | tf_op | source)
XLA Modules:
  0.0 464.6 jit_solution(17657803801040061868)
XLA Ops:
  0.7 1.7 slice_bitcast_fusion
  2.3 6.1 %concatenate.6 = bf16[384]{0:T(512)(128)(2,1)S(1)} concatenate(bf16[32]{0:T(256)(128)(2,1)} %param.19, bf16[32]{0:T(256)(128)(2,1)} %param.20, bf16[32]{0:T(256)(128)(2,1)} %param.22, bf16[32]{0:T(256)(128)(2,1)} %param.23, bf16[32]{0:T(256)(128)(2,1)} %param.25, bf16[32]{0:T(256)(128)(2,1)} %param.26, bf16[32]{0:T(256)(128)(2,1)} %param.27, bf16[32]{0:T(256)(128)(2,1)} %param.31, ...), dimensions={0} | concatenate | bytes 1536 | tf_op jit(solution)/shard_map/concatenate | solution.py:663
  8.4 0.6 broadcast_in_dim.2.refs_3_
  9.0 46.2 %spread_first.1 = (bf16[2,2,2,2,64,1024]{5,4,3,2,1,0:T(8,128)(2,1)}, bf16[2,2,2,2,64,1024]{5,4,3,2,1,0:T(8,128)(2,1)}, bf16[2,2,2,2,64,1024]{5,4,3,2,1,0:T(8,128)(2,1)}, bf16[2,2,2,2,8,768]{5,4,3,2,1,0:T(8,128)(2,1)}) custom-call(bf16[64,512]{1,0:T(8,128)(2,1)} %get-tuple-element.91.refs_0_, bf16[64,512]{1,0:T(8,128)(2,1)} %get-tuple-element.92.refs_1_, ...), custom_call_target="tpu_custom_call" | custom-call | tf_op jit(solution)/shard_map/spread_first/pallas_call | solution.py:403
  55.3 1.1 slice_reduce_fusion
  56.7 0.7 dynamic_slice.3
  57.5 1.7 multiply_reduce_fusion.6
  59.2 0.6 multiply_reduce_fusion.5
  60.0 1.9 copy.43
  62.0 1.6 add_convert_fusion.2
  63.5 2.4 copy.45.refs_0_
  66.0 0.7 reshape.348.refs_4_
  66.6 0.7 reshape.349.refs_5_
  67.3 0.6 compare_convert_fusion.refs_6_.refs_11_
  68.0 93.5 %attention.1 = (bf16[640,1024]{1,0:T(8,128)(2,1)}, bf16[640,1024]{1,0:T(8,128)(2,1)}, bf16[640,1024]{1,0:T(8,128)(2,1)}, bf16[640,1024]{1,0:T(8,128)(2,1)}, bf16...) custom-call(bf16[640,1024]{1,0:T(8,128)(2,1)} %copy.45.refs_0_, ...), custom_call_target="tpu_custom_call" | custom-call | tf_op jit(solution)/shard_map/attention/pallas_call | solution.py:403
  161.5 5.4 %fusion.18 = (f32[640]{0:T(1024)S(1)}, f32[640,1024]{0,1:T(8,128)}) fusion(f32[1024]{0:T(1024)S(1)} %reshape.350, bf16[640,1024]{1,0:T(8,128)(2,1)} %get-tuple-element.44.refs_3_, bf16[1024,1024]{1,0:T(8,128)(2,1)} %bitcast.106, f32[640,1024]{0,1:T(8,128)S(1)} %copy.43, f32[640]{0:T(1024)S(1)} %reshape.345), kind=kOutput, calls=%fused_computation.83 | convolution fusion | flops 1344798080 | bytes 8659968 | tf_op jit(solution)/shard_map/dot_general | solution.py:24
  167.0 2.2 multiply_reduce_fusion.4
  169.5 36.0 %multiply_convert_fusion = (bf16[640,4096]{1,0:T(8,128)(2,1)}, f32[640,4096]{1,0:T(8,128)}, f32[640,4096]{1,0:T(8,128)}) fusion(f32[4096]{0:T(1024)S(1)} %fusion.13, bf16[1024,4096]{1,0:T(8,128)(2,1)} %bitcast.123, f32[640,1024]{0,1:T(8,128)S(1)} %copy-done, f32[1024]{0:T(1024)S(1)} %reshape.352, f32[1024]{0:T(1024)S(1)} %reshape.351, ...), kind=kOutput, calls=%fused_computation.12 | convolution fusion | flops 5545000960 | bytes 37254144 | tf_op jit(solution)/shard_map/dot_general | solution.py:24
  205.6 11.9 %add_convert_fusion = bf16[640,1024]{0,1:T(8,128)(2,1)} fusion(f32[640,1024]{0,1:T(8,128)} %get-tuple-element.110, bf16[640,4096]{1,0:T(8,128)(2,1)} %get-tuple-element.88, bf16[1024,4096]{1,0:T(8,128)(2,1)} %bitcast.125, f32[1024]{0:T(1024)S(1)} %reshape.354), kind=kOutput, calls=%fused_computation.36 | convolution fusion | flops 5370675200 | bytes 17567744 | tf_op jit(solution)/shard_map/dot_general | solution.py:24
  217.5 2.4 copy.48
  219.9 16.1 %convert_reduce_fusion = (f32[4096]{0:T(1024)S(1)}, bf16[640,4096]{1,0:T(8,128)(2,1)S(1)}) fusion(f32[640,4096]{1,0:T(8,128)} %get-tuple-element.89, bf16[640,1024]{1,0:T(8,128)(2,1)} %bitcast.102, bf16[1024,4096]{1,0:T(8,128)(2,1)} %bitcast.126, f32[640,4096]{1,0:T(8,128)} %get-tuple-element.111, f32[4096]{0:T(1024)S(1)} %fusion.13), kind=kOutput, calls=%fused_computation.11 | convolution fusion | flops 5413269504 | bytes 35946496 | tf_op jit(solution)/shard_map/dot_general | solution.py:24
  236.1 11.0 %fusion.19 = (f32[1024]{0:T(1024)S(1)}, f32[640,1024]{1,0:T(8,128)}) fusion(bf16[640,4096]{1,0:T(8,128)(2,1)S(1)} %get-tuple-element.115, bf16[1024,4096]{1,0:T(8,128)(2,1)} %bitcast.124), kind=kOutput, calls=%fused_computation.84 | convolution fusion | flops 5369363456 | bytes 16257024 | tf_op jit(solution)/shard_map/dot_general | solution.py:24
  247.1 3.2 copy.50
  250.3 3.4 multiply_reduce_fusion
  253.7 2.6 copy.49
  256.3 5.0 %convert_reduce_fusion.2 = (f32[1024]{0:T(1024)S(1)}, bf16[640,1024]{0,1:T(8,128)(2,1)}) fusion(f32[640]{0:T(1024)S(1)} %get-tuple-element.116, f32[640,1024]{0,1:T(8,128)} %get-tuple-element.110, f32[640]{0:T(1024)S(1)} %broadcast_multiply_fusion.4, f32[640]{0:T(1024)S(1)} %get-tuple-element.117, f32[640,1024]{0,1:T(8,128)} %copy.50, ...), kind=kLoop, calls=%fused_computation.30 | loop fusion | flops 7863296 | bytes 7882752 | tf_op jit(solution)/shard_map/reduce_sum | solution.py:624
  261.3 2.5 copy.51.refs_4_
  263.8 1.6 fusion.32.refs_6_
  265.4 12.0 %convolution_convert_fusion.1 = bf16[4096,1024]{0,1:T(8,128)(2,1)} fusion(bf16[640,4096]{1,0:T(8,128)(2,1)} %get-tuple-element.88, bf16[640,1024]{1,0:T(8,128)(2,1)S(1)} %bitcast.104), kind=kOutput, calls=%fused_computation.27 | convolution fusion | flops 5372903424 | bytes 14942208 | tf_op jit(solution)/shard_map/dot_general | solution.py:24
  277.4 9.0 %convolution_convert_fusion = bf16[1024,4096]{1,0:T(8,128)(2,1)} fusion(bf16[640,4096]{1,0:T(8,128)(2,1)S(1)} %bitcast.128, f32[640,1024]{0,1:T(8,128)S(1)} %copy-done.1, f32[1024]{0:T(1024)S(1)} %reshape.352, f32[1024]{0:T(1024)S(1)} %reshape.351, f32[640]{0:T(1024)S(1)} %add_rsqrt_fusion, f32[640]{0:T(1024)S(1)} %broadcast_multiply_fusion.4), kind=kOutput, calls=%fused_computation.26 | convolution fusion | flops 5376180224 | bytes 16266240 | tf_op jit(solution)/shard_map/dot_general | solution.py:24
  286.5 95.7 %attention_back.1 = (bf16[1024,1024]{1,0:T(8,128)(2,1)}, bf16[1024,1024]{1,0:T(8,128)(2,1)}, bf16[1024,1024]{1,0:T(8,128)(2,1)}, bf16[1024,1024]{1,0:T(8,128)(2,...) custom-call(bf16[640,1024]{1,0:T(8,128)(2,1)} %get-tuple-element.48., ...), custom_call_target="tpu_custom_call" | custom-call | tf_op jit(solution)/shard_map/attention_back/pallas_call | solution.py:403
  382.2 3.4 copy.52
  385.6 2.8 multiply_reduce_fusion.1
  388.4 0.5 copy-done.3
  388.9 4.6 %add_multiply_fusion = f32[640,1024]{0,1:T(8,128)} fusion(f32[640,1024]{0,1:T(8,128)} %copy.52, f32[640]{0:T(1024)S(1)} %broadcast_multiply_fusion, f32[640]{0:T(1024)S(1)} %broadcast_multiply_fusion.1, f32[1024]{0:T(1024)S(1)} %reshape.346, f32[640]{0:T(1024)S(1)} %rsqrt.20, f32[640]{0:T(1024)S(1)} %reshape.345, f32[640]{0:T(1024)S(1)} %div.27, ...), kind=kLoop, calls=%fused_computation.32 | loop fusion | flops 12451840 | bytes 14449152 | tf_op jit(solution)/shard_map/mul | solution.py:734
  393.6 3.4 copy.53
  397.3 0.5 broadcast.277
  397.8 0.7 reduce.11
  398.5 0.7 reduce.12
  399.5 1.6 convert_reduce_fusion.1
  401.2 0.8 pad.4
  402.0 54.8 %fold_last.1 = (f32[64,512]{1,0:T(8,128)}, f32[64,512]{1,0:T(8,128)}, f32[64,512]{1,0:T(8,128)}, f32[8,384]{1,0:T(8,128)}, f32[64,512]{1,0:T(8,128)}) custom-call(bf16[2,2,2,2,64,1024]{5,4,3,2,1,0:T(8,128)(2,1)} %bitcast.109, bf16[2,2,2,2,64,1024]{5,4,3,2,1,0:T(8,128)(2,1)} %bitcast.110, bf16[2,2,2,2,64,1024]{5,4,3,2,1,0:T(8,128)(2,1)} %bitcast.111, ...), custom_call_target="tpu_custom_call" | custom-call | tf_op jit(solution)/shard_map/fold_last/pallas_call | solution.py:403
  456.8 1.4 slice_bitcast_fusion.4
  458.3 1.8 pad_maximum_fusion
  460.1 1.2 slice_bitcast_fusion.5
  461.3 1.6 copy.63
  462.9 0.8 copy.64
  463.6 0.8 copy.65
  (59 shorter events, 2.1 us)
Async XLA Ops:
  0.6 58.6 %copy-start.4 = (bf16[2,320,1024]{2,1,0:T(8,128)(2,1)S(1)}, bf16[2,320,1024]{2,1,0:T(8,128)(2,1)}, u32[]{:S(2)}) copy-start(bf16[2,320,1024]{2,1,0:T(8,128)(2,1)} %param.16) | copy-start | bytes 3932164
  167.0 2.5 copy-start
  236.1 11.0 %copy-start.11 = (bf16[640,4096]{1,0:T(8,128)(2,1)}, bf16[640,4096]{1,0:T(8,128)(2,1)S(1)}, u32[]{:S(2)}) copy-start(bf16[640,4096]{1,0:T(8,128)(2,1)S(1)} %get-tuple-element.115) | copy-start | bytes 15728644
  263.8 1.6 copy-start.6
  263.8 13.6 %slice-start = ((s8[5242880]{0:T(1024)(128)(4,1)}), s8[4194304]{0:T(1024)(128)(4,1)S(1)}, s32[]{:S(2)}) async-start(s8[5242880]{0:T(1024)(128)(4,1)} %bitcast.127), calls=%async_computation | async-start | bytes 8388608
  265.4 12.0 %copy-start.1 = (f32[640,1024]{0,1:T(8,128)S(1)}, f32[640,1024]{0,1:T(8,128)}, u32[]{:S(2)}) copy-start(f32[640,1024]{0,1:T(8,128)} %get-tuple-element.110) | copy-start | bytes 7864324
  265.4 12.0 %slice-start.1 = ((s8[5242880]{0:T(1024)(128)(4,1)}), s8[1048576]{0:T(1024)(128)(4,1)S(1)}, s32[]{:S(2)}) async-start(s8[5242880]{0:T(1024)(128)(4,1)} %bitcast.127), calls=%async_computation.1 | async-start | bytes 2097152
  385.6 2.9 copy-start.2
  385.6 3.3 copy-start.3
  393.6 3.4 copy-start.5
  396.9 0.8 copy-start.10
  396.9 1.6 copy-start.9
  402.0 60.8 %copy-start.8 = (f32[64,2048]{1,0:T(8,128)S(1)}, f32[64,2048]{1,0:T(8,128)}, u32[]{:S(2)}) copy-start(f32[64,2048]{1,0:T(8,128)} %get-tuple-element.144) | copy-start | bytes 1572868
  402.0 61.6 %copy-start.7 = (f32[64,2048]{1,0:T(8,128)S(1)}, f32[64,2048]{1,0:T(8,128)}, u32[]{:S(2)}) copy-start(f32[64,2048]{1,0:T(8,128)} %get-tuple-element.64) | copy-start | bytes 1572868
